TPU v7x, 256 devices: a whole 4x4x8 slice. The times are simulated.
256 devices in a mesh: tile: 32 (over z_lo, y, core), img: 8 (over x, z_hi).
Axes of the slice: x: 4, y: 4, z: 8 (z_hi: 2, z_lo: 4; z = z_hi * 4 + z_lo), core: 2. Of those that a mesh axis runs over, the one named last changes fastest.
Arguments:
- tower: bfloat16 [8, 64, 128, 256], P('img', 'tile'), may hold values from -6 to 6
- cls_weight: bfloat16 [720, 2304], replicated, may hold values from -0.125 to 0.125
- cls_bias: float32 [720], replicated, may hold values from -5.5 to -3.5
- box_weight: bfloat16 [36, 2304], replicated, may hold values from -0.125 to 0.125
- box_bias: float32 [36], replicated, may hold values from -0.5 to 0.5
- labels: int32 [8, 9, 64, 128], P('img', None, 'tile'), may hold values from -2 to 79, as said below
- target_index: int32 [8, 9, 64, 128], P('img', None, 'tile'), may hold values from 0 to 99
- boxes: float32 [8, 4, 100], P('img'), may hold values from -320 to 1344, as said below
Outputs:
- loss: float32 [], replicated
- cls_weight_grad: float32 [720, 2304], replicated
- cls_bias_grad: float32 [720], replicated
- box_weight_grad: float32 [36, 2304], replicated
- box_bias_grad: float32 [36], replicated
- tower_grad: bfloat16 [8, 64, 128, 256], P('img', 'tile')
Inputs may be any that keep to these rules, and one draw needn't show every extreme that they name: `labels`: -1 marks background and -2 an ignored anchor, other values are classes; every image has at least one anchor with a class. `boxes`: x1 < x2 and y1 < y2 in every box; sides between 8 and 640 pixels.
All inputs are finite; a program needn't handle non-finite values.
Results may differ from a plain program's by a relative error of at most 0.0053.
Values may be sent and summed in bfloat16 or wider, within the bound.
A program may use at most 64 MiB of HBM per device.

v0:
```python
import jax
import jax.numpy as jnp
from jax import lax
from jax.sharding import PartitionSpec as P

CLASSES = 80
ANCHORS = 9
STRIDE = 8


FOCAL_ALPHA = 0.25
NORM_EPS = 1e-06


def padded_2(value, sides, width):
    for axis, dim in sides:
        peers, length = (lax.axis_size(axis), value.shape[dim])
        up = [(i, (i + 1) % peers) for i in range(peers - 1)]
        down = [(j, i) for i, j in up]
        last = lax.slice_in_dim(value, length - width, length, axis=dim)
        initial = lax.slice_in_dim(value, 0, width, axis=dim)
        before = lax.ppermute(last, axis, up)
        after = lax.ppermute(initial, axis, down)
        value = jnp.concatenate([before, value, after], axis=dim)
    return value


def packed_total(arrays, axis):
    vector, at, gathered = (jnp.concatenate([a.reshape(-1) for a in arrays]), 0, [])
    subtotal = lax.psum(vector, axis)
    for a in arrays:
        gathered.append(subtotal[at : at + a.size].reshape(a.shape))
        at += a.size
    return tuple(gathered)


def build_patches(extended):
    rows_here = extended.shape[1] - 2
    columns = extended.shape[2]
    padded = jnp.pad(extended, ((0, 0), (0, 0), (1, 1), (0, 0)))
    pieces = []
    for row_tap in range(3):
        for col_tap in range(3):
            pieces.append(padded[:, row_tap : row_tap + rows_here, col_tap : col_tap + columns, :])
    return jnp.concatenate(pieces, axis=3)


def taps_back(dpatch, rows_lo, rows_out):
    images_here, rows_in, columns, width_all = dpatch.shape
    channels = width_all // 9
    pieces = dpatch.reshape(images_here, rows_in, columns, 9, channels)
    accumulated = jnp.zeros((images_here, rows_in + 2, columns + 2, channels), jnp.float32)
    for row_tap in range(3):
        for col_tap in range(3):
            accumulated = accumulated.at[
                :, row_tap : row_tap + rows_in, col_tap : col_tap + columns, :
            ].add(pieces[:, :, :, row_tap * 3 + col_tap, :])
    return accumulated[:, rows_lo : rows_lo + rows_out, 1 : columns + 1, :]


def head_terms(logits, deltas, labels, target_index, boxes, first_row):
    images_here = labels.shape[0]
    rows_here = labels.shape[2]
    columns = labels.shape[3]
    scores = logits.reshape(ANCHORS, CLASSES, images_here, rows_here, columns)
    assigned = jnp.transpose(labels, (1, 0, 2, 3))
    classes = lax.broadcasted_iota(jnp.int32, (1, CLASSES, 1, 1, 1), 1)
    target = (assigned[:, None] == classes).astype(jnp.float32)
    counted = (assigned >= -1).astype(jnp.float32)[:, None]
    probability = jax.nn.sigmoid(scores)
    hit_term = -FOCAL_ALPHA * (1.0 - probability) * (1.0 - probability) * jax.nn.log_sigmoid(scores)
    miss_term = -(1.0 - FOCAL_ALPHA) * probability * probability * jax.nn.log_sigmoid(-scores)
    focal_sum = jnp.sum(counted * (target * hit_term + (1.0 - target) * miss_term))
    offsets = deltas.reshape(ANCHORS, 4, images_here, rows_here, columns)
    anchor_ids = lax.broadcasted_iota(jnp.int32, (ANCHORS, 1, 1, 1), 0)
    scale_step = (anchor_ids // 3).astype(jnp.float32)
    ratio_step = (anchor_ids % 3 - 1).astype(jnp.float32)
    anchor_base = 4.0 * STRIDE * jnp.exp2(scale_step / 3.0)
    anchor_w = anchor_base * jnp.exp2(-ratio_step / 2.0)
    anchor_h = anchor_base * jnp.exp2(ratio_step / 2.0)
    row_ids = first_row + lax.broadcasted_iota(jnp.int32, (1, 1, rows_here, 1), 2)
    col_ids = lax.broadcasted_iota(jnp.int32, (1, 1, 1, columns), 3)
    centre_y = (row_ids.astype(jnp.float32) + 0.5) * STRIDE
    centre_x = (col_ids.astype(jnp.float32) + 0.5) * STRIDE
    middle_x = centre_x + offsets[:, 0] * anchor_w
    middle_y = centre_y + offsets[:, 1] * anchor_h
    pred_width = anchor_w * jnp.exp(offsets[:, 2])
    pred_height = anchor_h * jnp.exp(offsets[:, 3])
    pred_left = middle_x - 0.5 * pred_width
    pred_right = middle_x + 0.5 * pred_width
    pred_top = middle_y - 0.5 * pred_height
    pred_bottom = middle_y + 0.5 * pred_height
    flat_index = target_index.reshape(images_here, -1)
    picked = jnp.take_along_axis(
        boxes,
        jnp.broadcast_to(flat_index[:, None, :], (images_here, 4, flat_index.shape[1])),
        axis=2,
    )
    picked = jnp.transpose(
        picked.reshape(images_here, 4, ANCHORS, rows_here, columns), (1, 2, 0, 3, 4)
    )
    true_left, true_top, true_right, true_bottom = (picked[0], picked[1], picked[2], picked[3])
    crossing_w = jnp.maximum(
        jnp.minimum(pred_right, true_right) - jnp.maximum(pred_left, true_left), 0.0
    )
    crossing_h = jnp.maximum(
        jnp.minimum(pred_bottom, true_bottom) - jnp.maximum(pred_top, true_top), 0.0
    )
    crossing = crossing_w * crossing_h
    union_area = (
        pred_width * pred_height + (true_right - true_left) * (true_bottom - true_top) - crossing
    )
    outer_w = jnp.maximum(pred_right, true_right) - jnp.minimum(pred_left, true_left)
    outer_h = jnp.maximum(pred_bottom, true_bottom) - jnp.minimum(pred_top, true_top)
    outer_area = outer_w * outer_h
    giou_value = crossing / union_area - (outer_area - union_area) / outer_area
    positive = (assigned >= 0).astype(jnp.float32)
    giou_sum = jnp.sum(positive * (1.0 - giou_value))
    return (focal_sum, giou_sum)


def per_device(tower, cls_weight, cls_bias, box_weight, box_bias, labels, target_index, boxes):
    images_here = tower.shape[0]
    rows_here = tower.shape[1]
    columns = tower.shape[2]
    split_at = cls_weight.shape[0]
    weight_all = jnp.concatenate([cls_weight, box_weight], axis=0)
    bias_all = jnp.concatenate([cls_bias, box_bias])
    extended = padded_2(tower, (("tile", 1),), 1)
    patches = build_patches(extended)
    flat_patches = patches.reshape(-1, patches.shape[3])
    outputs = lax.dot_general(
        weight_all, flat_patches, (((1,), (1,)), ((), ())), preferred_element_type=jnp.float32
    )
    outputs = (outputs + bias_all[:, None]).reshape(
        weight_all.shape[0], images_here, rows_here, columns
    )
    first_row = lax.axis_index("tile") * rows_here

    def loss_pair(scores, offsets):
        return head_terms(scores, offsets, labels, target_index, boxes, first_row)

    loss_terms, pullback = jax.vjp(loss_pair, outputs[:split_at], outputs[split_at:])
    grad_scores, grad_offsets = pullback((jnp.ones((), jnp.float32), jnp.ones((), jnp.float32)))
    focal_local, giou_local = loss_terms
    count_local = jnp.sum((labels >= 0).astype(jnp.float32))
    grad_out = jnp.concatenate([grad_scores, grad_offsets], axis=0)
    grad_low = grad_out.astype(jnp.bfloat16)
    grad_flat = grad_low.reshape(grad_low.shape[0], -1)
    weight_terms = jnp.dot(grad_flat, flat_patches, preferred_element_type=jnp.float32)
    bias_terms = jnp.sum(grad_out, axis=(1, 2, 3))
    grad_rows = padded_2(grad_low, (("tile", 2),), 1)
    dpatch = lax.dot_general(
        grad_rows.reshape(grad_rows.shape[0], -1),
        weight_all,
        (((0,), (0,)), ((), ())),
        preferred_element_type=jnp.float32,
    )
    dpatch = dpatch.reshape(images_here, rows_here + 2, columns, weight_all.shape[1])
    tower_sum = taps_back(dpatch, 2, rows_here)
    tower_grad = tower_sum.astype(jnp.bfloat16)
    entries = weight_all.shape[0] * (weight_all.shape[1] + 1)
    focal_total, giou_total, positives, bias_sum = packed_total(
        (focal_local, giou_local, count_local, bias_terms), ("tile", "img")
    )
    weight_sum = lax.psum(weight_terms, ("tile", "img"))
    squares = jnp.sum(weight_sum * weight_sum) + jnp.sum(bias_sum * bias_sum)
    scale = lax.rsqrt(squares / entries + NORM_EPS)
    weight_norm = weight_sum * scale
    bias_norm = bias_sum * scale
    loss = (focal_total + giou_total) / positives
    return (
        loss,
        weight_norm[:split_at],
        bias_norm[:split_at],
        weight_norm[split_at:],
        bias_norm[split_at:],
        tower_grad,
    )


def solution(mesh):
    placed = (
        P("img", "tile", None, None),
        P(),
        P(),
        P(),
        P(),
        P("img", None, "tile", None),
        P("img", None, "tile", None),
        P("img", None, None),
    )
    return jax.shard_map(
        per_device,
        mesh=mesh,
        in_specs=placed,
        out_specs=(P(), P(), P(), P(), P(), P("img", "tile", None, None)),
        check_vma=False,
    )
```

profile of v0, /device:TPU:1, one launch (start us, length us, event | category | flops | bytes accessed | tf_op | source)
XLA Modules:
  0.0 430.4 jit_solution(16412508561127130968)
XLA Ops:
  7.2 1.5 fusion.90
  8.8 4.6 %collective-permute-start = (bf16[1,1,128,256]{3,2,1,0:T(8,128)(2,1)}, bf16[1,1,128,256]{3,2,1,0:T(8,128)(2,1)}, u32[]{:S(2)}, u32[]{:S(2)}) collective-permute-start(bf16[1,1,128,256]{3,2,1,0:T(8,128)(2,1)} %get-tuple-element.146), channel_id=1, source_target_pairs={{0,8},{8,16},{16,24},{24,32},{32,40},{40,48},{48,56},{56,64},{64,7... | collective-permute-start | bytes 196616 | tf_op jit(solution)/shard_map/ppermute | solution.py:22
  13.3 2.4 collective-permute-start.1
  18.9 1.3 compare_convert_fusion
  20.3 75.0 %gather_fusion = f32[9216]{0:T(1024)S(1)} fusion(f32[4,100]{1,0:T(4,128)S(1)} %bitcast.249, s32[9216]{0:T(1024)S(1)} %reshape.1606), kind=kCustom, calls=%fused_computation | custom fusion | bytes 147456 | tf_op jit(solution)/shard_map/jvp(jit(take_along_axis))/gather | solution.py:94
  95.4 2.2 constant_dynamic-update-slice_fusion.1
  97.6 3.6 copy.38
  101.2 1.4 and_reduce_fusion
  110.3 1.5 fusion.65
  113.7 10.4 %fusion.82 = (bf16[9,80,1,2,128]{4,3,1,0,2:T(2,128)(2,1)S(1)}, f32[9,80,1,2,128]{4,3,1,0,2:T(2,128)}, f32[]{:T(128)}) fusion(f32[9,80,1,2,128]{4,3,1,0,2:T(2,128)S(1)} %reshape.1582, f32[9,2,128]{2,1,0:T(2,128)S(1)} %copy-done.7, s32[9,2,128]{2,1,0:T(2,128)S(1)} %bitcast.269), kind=kLoop, calls=%fused_computation.207 | loop fusion | flops 12718079 | bytes 1861636 | tf_op jit(solution)/shard_map/convert.4
  124.2 1.4 copy.33
  125.6 4.0 convolution_bitcast_fusion
  129.8 3.1 collective-permute-start.2
  132.9 1.9 collective-permute-start.3
  135.6 2.0 pad_maximum_fusion.4
  137.6 83.6 %psum.14 = f32[759]{0:T(1024)S(1)} all-reduce(f32[759]{0:T(1024)S(1)} %pad_maximum_fusion.4), channel_id=1, replica_groups=mesh['tile'=32,'img'=8] {'tile','img'}, use_global_device_ids=true, to_apply=%region_4.6 | all-reduce | flops 759 | bytes 6072 | tf_op jit(solution)/shard_map/psum | solution.py:30
  224.4 4.0 convolution_bitcast_fusion.1
  228.6 2.1 copy-done.1
  230.7 1.3 fusion.35
  232.0 2.6 scatter-add.31
  234.6 3.0 add_select_fusion
  237.7 2.7 scatter-add.34
  240.4 1.2 fusion.34
  242.6 1.4 scatter-add.36
  245.2 1.4 scatter-add.39
  246.7 1.2 fusion.30
  249.0 1.4 scatter-add.41
  251.5 1.4 scatter-add.44
  253.6 154.0 %all-reduce.8.cloned.1.call-done = f32[756,2304]{1,0:T(8,128)} async-done(((f32[756,2304]{1,0:T(8,128)}), f32[756,2304]{1,0:T(8,128)}) %all-reduce.8.cloned.1.call-update) | async-done | bytes 6967312 | tf_op jit(solution)/shard_map/psum | solution.py:166
  407.6 5.4 %multiply_reduce_fusion = f32[]{:T(128)} fusion(f32[756,2304]{1,0:T(8,128)} %all-reduce.8.cloned.1.call-done), kind=kLoop, calls=%fused_computation.1 | loop fusion | flops 3483647 | bytes 6967300 | tf_op jit(solution)/shard_map/reduce_sum | solution.py:167
  414.4 3.4 broadcast_multiply_fusion
  418.6 3.2 slice.510
  (83 shorter events, 21.7 us)
Async XLA Ops:
  7.2 13.1 %copy-start = (f32[1,4,100]{2,1,0:T(4,128)S(1)}, f32[1,4,100]{2,1,0:T(4,128)}, u32[]{:S(2)}) copy-start(f32[1,4,100]{2,1,0:T(4,128)} %param.34) | copy-start | bytes 4804
  7.2 400.4 %all-reduce.8.cloned.1.call-start = ((), (), s32[]{:S(2)}) async-start(), calls=%async_computation | async-start | bytes 14008320 | tf_op jit(solution)/shard_map/psum | solution.py:166
  8.8 95.2 %collective-permute-start = (bf16[1,1,128,256]{3,2,1,0:T(8,128)(2,1)}, bf16[1,1,128,256]{3,2,1,0:T(8,128)(2,1)}, u32[]{:S(2)}, u32[]{:S(2)}) collective-permute-start(bf16[1,1,128,256]{3,2,1,0:T(8,128)(2,1)} %get-tuple-element.146), channel_id=1, source_target_pairs={{0,8},{8,16},{16,24},{24,32},{32,40},{40,48},{48,56},{56,64},{64,7... | collective-permute-start | bytes 196616 | tf_op jit(solution)/shard_map/ppermute | solution.py:22
  13.3 90.6 %collective-permute-start.1 = (bf16[1,1,128,256]{3,2,1,0:T(8,128)(2,1)}, bf16[1,1,128,256]{3,2,1,0:T(8,128)(2,1)}, u32[]{:S(2)}, u32[]{:S(2)}) collective-permute-start(bf16[1,1,128,256]{3,2,1,0:T(8,128)(2,1)} %get-tuple-element.147), channel_id=1, source_target_pairs={{8,0},{16,8},{24,16},{32,24},{40,32},{48,40},{56,48},{64,56},{72,6... | collective-permute-start | bytes 196616 | tf_op jit(solution)/shard_map/ppermute | solution.py:23
  16.4 3.9 copy-start.8
  95.3 2.3 copy-start.4
  107.8 1.2 copy-start.2
  109.0 4.4 %copy-start.6 = (f32[9]{0:T(128)S(1)}, f32[9]{0:T(128)}, u32[]{:S(2)}) copy-start(f32[9]{0:T(128)} %get-tuple-element.161) | copy-start | bytes 112
  109.0 4.7 %copy-start.5 = (s32[1,9,2,128]{3,2,1,0:T(2,128)S(1)}, s32[1,9,2,128]{3,2,1,0:T(2,128)}, u32[]{:S(2)}) copy-start(s32[1,9,2,128]{3,2,1,0:T(2,128)} %param.32) | copy-start | bytes 27652
  109.0 4.7 %copy-start.7 = (f32[9,2,128]{2,1,0:T(2,128)S(1)}, f32[9,2,128]{2,1,0:T(2,128)}, u32[]{:S(2)}) copy-start(f32[9,2,128]{2,1,0:T(2,128)} %compare_convert_fusion) | copy-start | bytes 27652
  109.1 16.5 %copy-start.3 = (bf16[1,2,128,2304]{3,2,1,0:T(8,128)(2,1)S(1)}, bf16[1,2,128,2304]{3,2,1,0:T(8,128)(2,1)}, u32[]{:S(2)}) copy-start(bf16[1,2,128,2304]{3,2,1,0:T(8,128)(2,1)} %copy-done.2) | copy-start | bytes 3538948
  129.8 94.6 %collective-permute-start.2 = (bf16[756,1,1,128]{0,3,2,1:T(8,128)(2,1)S(1)}, bf16[756,1,1,128]{0,3,2,1:T(8,128)(2,1)S(1)}, u32[]{:S(2)}, u32[]{:S(2)}) collective-permute-start(bf16[756,1,1,128]{0,3,2,1:T(8,128)(2,1)S(1)} %get-tuple-element.144), channel_id=1, source_target_pairs={{0,8},{8,16},{16,24},{24,32},{32,40},{40,48},{48,56},{56,64},{64,7... | collective-permute-start | bytes 580616 | tf_op jit(solution)/shard_map/ppermute | solution.py:22
  132.9 91.5 %collective-permute-start.3 = (bf16[756,1,1,128]{0,3,2,1:T(8,128)(2,1)S(1)}, bf16[756,1,1,128]{0,3,2,1:T(8,128)(2,1)S(1)}, u32[]{:S(2)}, u32[]{:S(2)}) collective-permute-start(bf16[756,1,1,128]{0,3,2,1:T(8,128)(2,1)S(1)} %get-tuple-element.145), channel_id=1, source_target_pairs={{8,0},{16,8},{24,16},{32,24},{40,32},{48,40},{56,48},{64,56},{72,6... | collective-permute-start | bytes 580616 | tf_op jit(solution)/shard_map/ppermute | solution.py:23
  228.5 2.2 copy-start.1
  414.4 7.5 %copy-start.9 = (f32[756]{0:T(1024)}, f32[756]{0:T(1024)S(1)}, u32[]{:S(2)}) copy-start(f32[756]{0:T(1024)S(1)} %slice_multiply_fusion) | copy-start | bytes 9076
Sparse Core Ops, SparseCore 0:
  129.8 277.7 all-reduce.7
where the time goes:
time: 433 us; the launch traced here: 430 us
  waiting for transfers between devices  154 us (36%)
  local copies, waits for them, and re-layouts  107 us (25%)
  blocking collectives  83.6 us (19%)
  other arithmetic  46 us (11%)
  between operations  19 us (4%)
  starting transfers between devices  12.1 us (3%)
  matrix products  9.22 us (2%)
    psum x1, waiting for transfers between devices, per_device(): weight_sum = lax.psum(weight_terms, ('tile', 'img'))  154 us
    psum x1, blocking collectives, packed_total(): subtotal = lax.psum(vector, axis)  83.6 us
    gather x3, local copies, waits for them, and re-layouts, head_terms(): jnp.take_along_axis(boxes, jnp.broadcast_to(flat_index[:, None, :], (imag...  75 us
    another operation x5, other arithmetic  14.9 us
    scatter-add x7, local copies, waits for them, and re-layouts, taps_back(): accumulated = accumulated.at[:, row_tap:row_tap + rows_in, col_tap:col_ta...  11.1 us
  transfers between devices with their start and end apart: 5, of which 1 were waited for; matrix products, arithmetic and copies ran while one was open for 28% of the time, Pallas kernels for 0%

commit v1 on v0

v1 whole, which is shorter than its diff:
```python
import functools

import jax
import jax.numpy as jnp
import numpy as np
from jax import lax
from jax.experimental import pallas as pl
from jax.experimental.pallas import tpu as pltpu
from jax.sharding import PartitionSpec as P

CLASSES = 80
ANCHORS = 9
STRIDE = 8
FOCAL_ALPHA = 0.25
NORM_EPS = 1e-06

RING = 4
CLS = ANCHORS * CLASSES
OUTS = CLS + 4 * ANCHORS
PAD_OUTS = 768
TAPS = 9
DEPTH = 256
WIDTH = TAPS * DEPTH
HALF = WIDTH // 2
COLS = 128
BLOCK = PAD_OUTS // (RING * RING)
SPLIT = 640
BF16 = jnp.bfloat16
F32 = jnp.float32
MESH = pl.DeviceIdType.MESH


def flip(i):
    return i + 1 - 2 * (i % 2)


class Links:
    def __init__(self, send, recv):
        self.send, self.recv, self.used, self.sent = send, recv, 0, []

    def make(self, src, dst, device):
        i = self.used
        self.used += 1
        return pltpu.make_async_remote_copy(
            src_ref=src,
            dst_ref=dst,
            send_sem=self.send.at[i],
            recv_sem=self.recv.at[i],
            device_id=device,
            device_id_type=MESH,
        )

    def push(self, src, dst, device):
        copy = self.make(src, dst, device)
        copy.start()
        self.sent.append(copy)
        return copy

    def drain(self):
        for copy in self.sent:
            copy.wait_send()


def anchor_sizes():
    ids = np.arange(ANCHORS)
    base = np.float32(4.0 * STRIDE) * np.exp2((ids // 3).astype(np.float32) / np.float32(3.0))
    ratio = (ids % 3 - 1).astype(np.float32) / np.float32(2.0)
    return (base * np.exp2(-ratio)).astype(np.float32), (base * np.exp2(ratio)).astype(np.float32)


def box_terms(offsets, assigned, corners, first_row):
    shape = assigned.shape
    ids = lax.broadcasted_iota(jnp.int32, shape, 0)
    lanes = lax.broadcasted_iota(jnp.int32, shape, 1)
    widths, heights = anchor_sizes()
    anchor_w = jnp.zeros(shape, F32)
    anchor_h = jnp.zeros(shape, F32)
    for a in range(ANCHORS):
        anchor_w = jnp.where(ids == a, float(widths[a]), anchor_w)
        anchor_h = jnp.where(ids == a, float(heights[a]), anchor_h)
    second = (lanes >= COLS).astype(jnp.int32)
    centre_y = ((first_row + second).astype(F32) + 0.5) * STRIDE
    centre_x = ((lanes - COLS * second).astype(F32) + 0.5) * STRIDE
    true_left, true_top, true_right, true_bottom = corners
    positive = (assigned >= 0).astype(F32)

    def each(o0, o1, o2, o3):
        middle_x = centre_x + o0 * anchor_w
        middle_y = centre_y + o1 * anchor_h
        pred_width = anchor_w * jnp.exp(o2)
        pred_height = anchor_h * jnp.exp(o3)
        pred_left = middle_x - 0.5 * pred_width
        pred_right = middle_x + 0.5 * pred_width
        pred_top = middle_y - 0.5 * pred_height
        pred_bottom = middle_y + 0.5 * pred_height
        crossing_w = jnp.maximum(
            jnp.minimum(pred_right, true_right) - jnp.maximum(pred_left, true_left), 0.0
        )
        crossing_h = jnp.maximum(
            jnp.minimum(pred_bottom, true_bottom) - jnp.maximum(pred_top, true_top), 0.0
        )
        crossing = crossing_w * crossing_h
        union_area = (
            pred_width * pred_height
            + (true_right - true_left) * (true_bottom - true_top)
            - crossing
        )
        outer_w = jnp.maximum(pred_right, true_right) - jnp.minimum(pred_left, true_left)
        outer_h = jnp.maximum(pred_bottom, true_bottom) - jnp.minimum(pred_top, true_top)
        outer_area = outer_w * outer_h
        giou_value = crossing / union_area - (outer_area - union_area) / outer_area
        return positive * (1.0 - giou_value)

    values, pullback = jax.vjp(each, *offsets)
    return values, pullback(jnp.ones(shape, F32)), positive


def shifted(value, tap):
    if tap == 1:
        return value
    rows = lax.broadcasted_iota(jnp.int32, value.shape, 0)
    if tap == 0:
        return jnp.where(rows == 0, 0.0, pltpu.roll(value, 1, 0))
    return jnp.where(rows == COLS - 1, 0.0, pltpu.roll(value, COLS - 1, 0))


def step_kernel(
    zl_count, zh_count,
    tower, wc_hbm, wb, bias, labels, tindex, boxes,
    r_out, s_out, tg_out,
    w, wbs, patches, halo, outs, gf, glow, boxy, acc, send_c, recv_c,
    a1s, a1r, a2s, a2r, accb, b1s0, b1r0, b2s0, b2r0, b1s1, b1r1, b2s1, b2r1,
    zf, zs, zr, zg, sc, sx, sy, sz, dpatch, edge_s, edge_r,
    wsem, send, recv,
):
    t = lax.axis_index("tile")
    m = lax.axis_index("img")
    tiles = zl_count * RING * 2
    nz = zl_count * zh_count
    c = t % 2
    y = (t // 2) % RING
    x = m // zh_count
    z = (m % zh_count) * zl_count + t // (2 * RING)

    def at(x_, y_, z_, c_):
        return {
            "tile": (z_ % zl_count) * (2 * RING) + y_ * 2 + c_,
            "img": x_ * zh_count + z_ // zl_count,
        }

    a = x + c * (y - x)
    b = y + c * (x - y)

    def ring(a_, b_):
        return at(a_ + c * (b_ - a_), b_ + c * (a_ - b_), z, c)

    sibling = at(x, y, z, 1 - c)
    above = {"tile": t - 1, "img": m}
    below = {"tile": t + 1, "img": m}
    links = Links(send, recv)

    load = pltpu.make_async_copy(wc_hbm, w, wsem)
    load.start()

    barrier = pltpu.get_barrier_semaphore()

    def greet(device):
        pl.semaphore_signal(barrier, inc=1, device_id=device, device_id_type=MESH)

    greet(sibling)
    for k in range(1, RING):
        greet(at((x + k) % RING, y, z, c))
        greet(at(x, (y + k) % RING, z, c))
    for k in range(1, nz):
        greet(at(x, y, (z + k) % nz, c))

    @pl.when(t > 0)
    def _():
        greet(above)

    @pl.when(t < tiles - 1)
    def _():
        greet(below)

    wanted = jnp.concatenate([tindex[0, :, 0, :], tindex[0, :, 1, :]], axis=1)

    def pick(n, found):
        hit = wanted == n
        return tuple(jnp.where(hit, boxes[0, j, n], found[j]) for j in range(4))

    zero = jnp.zeros(wanted.shape, F32)
    corners = lax.fori_loop(0, boxes.shape[2], pick, (zero, zero, zero, zero))
    wbs[...] = jnp.zeros(wbs.shape, BF16)
    wbs[0 : 4 * ANCHORS, :] = wb[...]

    def fill(row, ext):
        value = row.astype(F32)
        for col_tap in range(3):
            piece = shifted(value, col_tap).astype(BF16)
            for here in range(2):
                row_tap = ext - here
                if 0 <= row_tap <= 2:
                    for part in range(2):
                        k = (3 * row_tap + col_tap) * DEPTH + part * COLS
                        patches[k // HALF, here * COLS : (here + 1) * COLS,
                                k % HALF : k % HALF + COLS] = piece[:, part * COLS : (part + 1) * COLS]

    fill(tower[0, 0], 1)
    fill(tower[0, 1], 2)

    greeted = 1 + 2 * (RING - 1) + nz - 1
    pl.semaphore_wait(
        barrier, greeted + (t > 0).astype(jnp.int32) + (t < tiles - 1).astype(jnp.int32)
    )

    halo_up = links.make(tower.at[0, 0], halo.at[1], above)
    halo_down = links.make(tower.at[0, 1], halo.at[0], below)

    @pl.when(t > 0)
    def _():
        halo_up.start()

    @pl.when(t < tiles - 1)
    def _():
        halo_down.start()

    @pl.when(t == 0)
    def _():
        halo[0] = jnp.zeros(halo.shape[1:], BF16)

    @pl.when(t == tiles - 1)
    def _():
        halo[1] = jnp.zeros(halo.shape[1:], BF16)

    load.wait()

    @pl.when(t < tiles - 1)
    def _():
        halo_up.wait_recv()

    @pl.when(t > 0)
    def _():
        halo_down.wait_recv()

    fill(halo[0], 0)
    fill(halo[1], 3)

    nt = (((1,), (1,)), ((), ()))

    def product(lhs, rhs):
        return lax.dot_general(lhs, rhs, nt, preferred_element_type=F32)

    bias_col = jnp.transpose(jnp.broadcast_to(bias[...], (8, PAD_OUTS)))[:, 0:1]
    outs[0:CLS, :] = (
        product(w[:, 0:HALF], patches[0]) + product(w[:, HALF:WIDTH], patches[1]) + bias_col[0:CLS]
    )
    outs[CLS:PAD_OUTS, :] = (
        product(wbs[:, 0:HALF], patches[0])
        + product(wbs[:, HALF:WIDTH], patches[1])
        + bias_col[CLS:PAD_OUTS]
    )

    class_ids = lax.broadcasted_iota(jnp.int32, (CLASSES, COLS), 0)

    def focal(anchor, total):
        rows = pl.ds(pl.multiple_of(anchor * CLASSES, CLASSES), CLASSES)
        for here in range(2):
            lanes = slice(here * COLS, (here + 1) * COLS)
            score = outs[rows, lanes]
            label = labels[0, anchor, here : here + 1, :]
            hit = jnp.broadcast_to(label, (CLASSES, COLS)) == class_ids
            counted = (label >= -1).astype(F32)
            side = jnp.where(hit, score, -score)
            small = jnp.exp(-jnp.abs(score))
            inverse = 1.0 / (1.0 + small)
            log_p = jnp.minimum(side, 0.0) - jnp.log1p(small)
            right = side >= 0
            p = jnp.where(right, inverse, small * inverse)
            miss = jnp.where(right, small * inverse, inverse)
            alpha = jnp.where(hit, FOCAL_ALPHA, FOCAL_ALPHA - 1.0) * counted
            weight = alpha * miss * miss
            grad = weight * (2.0 * p * log_p - miss)
            value = -jnp.abs(weight) * log_p
            gf[rows, lanes] = grad
            glow[rows, lanes] = grad.astype(BF16)
            total = total + jnp.sum(value.reshape(CLASSES // 8, 8, COLS), axis=0)
        return total

    focal_sum = lax.fori_loop(0, ANCHORS, focal, jnp.zeros((8, COLS), F32))

    assigned = jnp.concatenate([labels[0, :, 0, :], labels[0, :, 1, :]], axis=1)
    for here in range(2):
        boxy[here] = outs[CLS:PAD_OUTS, here * COLS : (here + 1) * COLS]
    offsets = [
        jnp.concatenate([boxy[here, pl.ds(j, ANCHORS, stride=4), :] for here in range(2)], axis=1)
        for j in range(4)
    ]
    giou, offset_grads, positive = box_terms(offsets, assigned, corners, 2 * t)
    boxy[...] = jnp.zeros(boxy.shape, F32)
    for here in range(2):
        lanes = slice(here * COLS, (here + 1) * COLS)
        for j in range(4):
            boxy[here, pl.ds(j, ANCHORS, stride=4), :] = offset_grads[j][:, lanes]
        gf[CLS:PAD_OUTS, lanes] = boxy[here]
    glow[CLS:PAD_OUTS, :] = gf[CLS:PAD_OUTS, :].astype(BF16)

    send_to_core = []
    for k in range(RING):
        rows = slice(k * RING * BLOCK, (k + 1) * RING * BLOCK)
        part = jnp.dot(glow[rows, :], patches[1 - c], preferred_element_type=F32)
        send_c[k] = part.astype(BF16).reshape(RING, BLOCK, HALF)
        send_to_core.append(links.push(send_c.at[k], recv_c.at[k], sibling))

    sums = lax.dot_general(
        jnp.ones((8, 2 * COLS), F32), gf[...], nt,
        precision=lax.Precision.HIGHEST, preferred_element_type=F32,
    )
    lane = lax.broadcasted_iota(jnp.int32, (1, COLS), 1)
    mine = jnp.zeros((8, COLS), F32)
    rows8 = lax.broadcasted_iota(jnp.int32, (8, COLS), 0)
    for k in range(PAD_OUTS // COLS):
        mine = jnp.where(rows8 == k, sums[:, k * COLS : (k + 1) * COLS], mine)
    scalars = (jnp.sum(focal_sum), jnp.sum(giou), jnp.sum(positive))
    for k, value in enumerate(scalars):
        mine = jnp.where((rows8 == 6) & (lane == k), value, mine)
    sc[c] = mine
    small_c = links.push(sc.at[c], sc.at[c], sibling)

    def own(k, carry):
        rows = pl.ds(pl.multiple_of(k * RING * BLOCK, RING * BLOCK), RING * BLOCK)
        part = jnp.dot(glow[rows, :], patches[c], preferred_element_type=F32)
        acc[k] = part.reshape(RING, BLOCK, HALF)
        return carry

    lax.fori_loop(0, RING, own, 0)

    small_c.wait_recv()
    sx[x] = sc[0] + sc[1]
    small_x = [
        links.push(sx.at[x], sx.at[x], at((x + k) % RING, y, z, c)) for k in range(1, RING)
    ]
    for copy in send_to_core:
        copy.wait_recv()

    def pair(quarter, j):
        return acc[quarter, j] + recv_c[quarter, j].astype(F32)

    steps_a = ((flip(a), 3 - a), (3 - a, flip(a)))
    first = {}
    for which in (1, 0):
        for s in range(2):
            near, far = steps_a[s]
            back = (3 - near, flip(near))[s]
            quarter = back if which else near
            for j in range(2):
                a1s[s, which, j] = pair(quarter, 2 * s + j).astype(BF16)
            first[s, which] = links.push(a1s.at[s, which], a1r.at[s, which], ring(near, b))

    tn = (((0,), (0,)), ((), ()))
    dpatch[...] = lax.dot_general(
        glow[0:CLS, :], w[...], tn, preferred_element_type=F32
    ) + lax.dot_general(glow[CLS:PAD_OUTS, :], wbs[...], tn, preferred_element_type=F32)

    def reach(row_tap, here):
        total = None
        for col_tap in range(3):
            k = (3 * row_tap + col_tap) * DEPTH
            piece = shifted(dpatch[here * COLS : (here + 1) * COLS, k : k + DEPTH], 2 - col_tap)
            total = piece if total is None else total + piece
        return total

    edge_s[0] = reach(0, 0)
    edge_s[1] = reach(2, 1)
    edge_up = links.make(edge_s.at[0], edge_r.at[1], above)
    edge_down = links.make(edge_s.at[1], edge_r.at[0], below)

    @pl.when(t > 0)
    def _():
        edge_up.start()

    @pl.when(t < tiles - 1)
    def _():
        edge_down.start()

    @pl.when(t == 0)
    def _():
        edge_r[0] = jnp.zeros(edge_r.shape[1:], F32)

    @pl.when(t == tiles - 1)
    def _():
        edge_r[1] = jnp.zeros(edge_r.shape[1:], F32)

    second = []
    for s in range(2):
        near, far = steps_a[s]
        first[s, 1].wait_recv()
        for j in range(2):
            a2s[s, j] = (pair(far, 2 * s + j) + a1r[s, 1, j].astype(F32)).astype(BF16)
        second.append(links.push(a2s.at[s], a2r.at[s], ring(far, b)))

    for copy in small_x:
        copy.wait_recv()
    sy[y] = (sx[0] + sx[1]) + (sx[2] + sx[3])
    small_y = [
        links.push(sy.at[y], sy.at[y], at(x, (y + k) % RING, z, c)) for k in range(1, RING)
    ]

    tg_own = (reach(1, 0) + reach(0, 1), reach(2, 0) + reach(1, 1))

    @pl.when(t < tiles - 1)
    def _():
        edge_up.wait_recv()

    @pl.when(t > 0)
    def _():
        edge_down.wait_recv()

    for here in range(2):
        tg_out[0, here] = (tg_own[here] + edge_r[here]).astype(BF16)

    for s in range(2):
        first[s, 0].wait_recv()
        second[s].wait_recv()
        for j in range(2):
            accb[2 * s + j] = (
                pair(a, 2 * s + j) + a1r[s, 0, j].astype(F32) + a2r[s, j].astype(F32)
            )

    steps_b = ((flip(b), 3 - b), (3 - b, flip(b)))
    bufs = ((b1s0, b1r0, b2s0, b2r0, slice(0, SPLIT)), (b1s1, b1r1, b2s1, b2r1, slice(SPLIT, HALF)))
    first = {}
    for which in (1, 0):
        for s in range(2):
            near, far = steps_b[s]
            back = (3 - near, flip(near))[s]
            quarter = back if which else near
            s1, r1, s2, r2, cols = bufs[s]
            s1[which] = accb[quarter, :, cols].astype(BF16)
            first[s, which] = links.push(s1.at[which], r1.at[which], ring(a, near))
    second = []
    for s in range(2):
        near, far = steps_b[s]
        s1, r1, s2, r2, cols = bufs[s]
        first[s, 1].wait_recv()
        s2[...] = (accb[far, :, cols] + r1[1].astype(F32)).astype(BF16)
        second.append(links.push(s2, r2, ring(a, far)))
    for copy in small_y:
        copy.wait_recv()
    sz[z] = (sy[0] + sy[1]) + (sy[2] + sy[3])
    small_z = [
        links.push(sz.at[z], sz.at[z], at(x, y, (z + k) % nz, c)) for k in range(1, nz)
    ]
    per = zf.shape[1] // 8
    groups = BLOCK // 8
    zf[...] = jnp.zeros(zf.shape, F32)
    for s in range(2):
        s1, r1, s2, r2, cols = bufs[s]
        first[s, 0].wait_recv()
        second[s].wait_recv()
        done = accb[b, :, cols] + r1[0].astype(F32) + r2[...].astype(F32)
        for k in range(cols.start // COLS, cols.stop // COLS):
            at_col = k * COLS - cols.start
            for g in range(groups):
                n = k * groups + g
                zf[n // per, (n % per) * 8 : (n % per) * 8 + 8, :] = done[
                    g * 8 : g * 8 + 8, at_col : at_col + COLS
                ]

    zs[...] = zf[...].astype(BF16)
    turns = [
        links.push(zs.at[(z + k) % nz], zr.at[z], at(x, y, (z + k) % nz, c)) for k in range(1, nz)
    ]
    total = zf[z]
    for k in range(1, nz):
        turns[k - 1].wait_recv()
        total = total + zr[(z + nz - k) % nz].astype(F32)
    zg[z] = total.astype(BF16)
    turns = [
        links.push(zg.at[z], zg.at[z], at(x, y, (z + k) % nz, c)) for k in range(1, nz)
    ]
    for copy in turns:
        copy.wait_recv()
    zf[...] = zg[...].astype(F32)
    for k in range(HALF // COLS):
        pieces = []
        for g in range(groups):
            n = k * groups + g
            pieces.append(zf[n // per, (n % per) * 8 : (n % per) * 8 + 8, :])
        r_out[c, a, b, :, k * COLS : (k + 1) * COLS] = jnp.concatenate(pieces, axis=0).astype(BF16)

    def wrap(i):
        return (i + RING) % RING

    top, bottom = slice(0, 32), slice(32, BLOCK)
    shared = []

    def share(a_, b_):
        shared.append(links.push(r_out.at[c, a_, b_], r_out.at[c, a_, b_], sibling))

    def along_a(b_):
        block = r_out.at[c, a, b_]
        return (
            links.push(block, block, ring(wrap(a + 1), b)),
            links.push(block, block, ring(wrap(a - 1), b)),
        )

    block = r_out.at[c, a, b]
    to_next = links.push(block, block, ring(a, wrap(b + 1)))
    to_last = links.push(block, block, ring(a, wrap(b - 1)))
    wide = [along_a(b)]
    share(a, b)
    to_next.wait_recv()
    block = r_out.at[c, a, wrap(b - 1), top]
    on_next = links.push(block, block, ring(a, wrap(b + 1)))
    wide.append(along_a(wrap(b - 1)))
    share(a, wrap(b - 1))
    to_last.wait_recv()
    block = r_out.at[c, a, wrap(b + 1), bottom]
    on_last = links.push(block, block, ring(a, wrap(b - 1)))
    wide.append(along_a(wrap(b + 1)))
    share(a, wrap(b + 1))
    on_next.wait_recv()
    on_last.wait_recv()
    wide.append(along_a(wrap(b + 2)))
    share(a, wrap(b + 2))

    order = (b, wrap(b - 1), wrap(b + 1), wrap(b + 2))
    rest = []
    for k, b_ in enumerate(order):
        wide[k][0].wait_recv()
        if k < 2:
            block = r_out.at[c, wrap(a - 1), b_]
            rest.append(links.push(block, block, ring(wrap(a + 1), b)))
        share(wrap(a - 1), b_)
        wide[k][1].wait_recv()
        if k >= 2:
            block = r_out.at[c, wrap(a + 1), b_]
            rest.append(links.push(block, block, ring(wrap(a - 1), b)))
        share(wrap(a + 1), b_)
    for k, b_ in enumerate(order):
        rest[k].wait_recv()
        share(wrap(a + 2), b_)

    for copy in small_z:
        copy.wait_recv()
    whole = sz[0]
    for k in range(1, nz):
        whole = whole + sz[k]
    s_out[...] = whole

    for copy in shared:
        copy.wait_recv()
    links.drain()

    @pl.when(t > 0)
    def _():
        halo_up.wait_send()
        edge_up.wait_send()

    @pl.when(t < tiles - 1)
    def _():
        halo_down.wait_send()
        edge_down.wait_send()


def scale_kernel(r, s, cls_out, box_out, bias_out, stage, sem):
    def squares(k, total):
        for h in range(2):
            value = r[h, k // RING, k % RING].astype(F32)
            value = value * value
            value = jnp.sum(value.reshape(BLOCK // 8, 8, HALF), axis=0)
            for j in range(HALF // COLS):
                total = total + value[:, j * COLS : (j + 1) * COLS]
        return total

    total = lax.fori_loop(0, RING * RING, squares, jnp.zeros((8, COLS), F32))
    rows8 = lax.broadcasted_iota(jnp.int32, (8, COLS), 0)
    bias = jnp.where(rows8 < PAD_OUTS // COLS, s[...], 0.0)
    total = jnp.sum(total + bias * bias, keepdims=True)
    scale = lax.rsqrt(total / (OUTS * (WIDTH + 1)) + NORM_EPS)
    bias_out[...] = bias * scale

    slots = stage.shape[0]
    count = CLS // BLOCK

    def store(k):
        return pltpu.make_async_copy(
            stage.at[k % slots],
            cls_out.at[pl.ds(pl.multiple_of(k * BLOCK, BLOCK), BLOCK)],
            sem.at[k % slots],
        )

    def chunk(k, carry):
        @pl.when(k >= slots)
        def _():
            store(k - slots).wait()

        for h in range(2):
            stage[k % slots, :, h * HALF : (h + 1) * HALF] = (
                r[h, k // RING, k % RING].astype(F32) * scale
            )
        store(k).start()
        return carry

    lax.fori_loop(0, count, chunk, 0)
    for h in range(2):
        box_out[:, h * HALF : (h + 1) * HALF] = (
            r[h, RING - 1, RING - 1].astype(F32) * scale
        )[0 : 4 * ANCHORS]
    for k in range(count - slots, count):
        store(k).wait()


def per_device(
    zl_count, zh_count, tower, cls_weight, cls_bias, box_weight, box_bias, labels, target_index, boxes
):
    nz = zl_count * zh_count
    tiles8 = BLOCK // 8 * (HALF // COLS)
    per = -(-tiles8 // nz) * 8
    bias = jnp.concatenate([cls_bias, box_bias, jnp.zeros((PAD_OUTS - OUTS,), F32)])[None]
    vmem = pl.BlockSpec(memory_space=pltpu.VMEM)
    copies = 100 + 4 * nz

    def buf(*shape, dtype=BF16):
        return pltpu.VMEM(shape, dtype)

    r, s, tower_grad = pl.pallas_call(
        functools.partial(step_kernel, zl_count, zh_count),
        out_shape=(
            jax.ShapeDtypeStruct((2, RING, RING, BLOCK, HALF), BF16),
            jax.ShapeDtypeStruct((8, COLS), F32),
            jax.ShapeDtypeStruct(tower.shape, BF16),
        ),
        in_specs=[
            vmem,
            pl.BlockSpec(memory_space=pl.ANY),
            vmem, vmem, vmem, vmem,
            pl.BlockSpec(memory_space=pltpu.SMEM),
        ],
        out_specs=(vmem, vmem, vmem),
        scratch_shapes=[
            buf(CLS, WIDTH),
            buf(PAD_OUTS - CLS, WIDTH),
            buf(2, 2 * COLS, HALF),
            buf(2, COLS, DEPTH),
            buf(PAD_OUTS, 2 * COLS, dtype=F32),
            buf(PAD_OUTS, 2 * COLS, dtype=F32),
            buf(PAD_OUTS, 2 * COLS),
            buf(2, PAD_OUTS - CLS, COLS, dtype=F32),
            buf(RING, RING, BLOCK, HALF, dtype=F32),
            buf(RING, RING, BLOCK, HALF),
            buf(RING, RING, BLOCK, HALF),
            buf(2, 2, 2, BLOCK, HALF),
            buf(2, 2, 2, BLOCK, HALF),
            buf(2, 2, BLOCK, HALF),
            buf(2, 2, BLOCK, HALF),
            buf(RING, BLOCK, HALF, dtype=F32),
            buf(2, BLOCK, SPLIT),
            buf(2, BLOCK, SPLIT),
            buf(BLOCK, SPLIT),
            buf(BLOCK, SPLIT),
            buf(2, BLOCK, HALF - SPLIT),
            buf(2, BLOCK, HALF - SPLIT),
            buf(BLOCK, HALF - SPLIT),
            buf(BLOCK, HALF - SPLIT),
            buf(nz, per, COLS, dtype=F32),
            buf(nz, per, COLS),
            buf(nz, per, COLS),
            buf(nz, per, COLS),
            buf(2, 8, COLS, dtype=F32),
            buf(RING, 8, COLS, dtype=F32),
            buf(RING, 8, COLS, dtype=F32),
            buf(nz, 8, COLS, dtype=F32),
            buf(2 * COLS, WIDTH, dtype=F32),
            buf(2, COLS, DEPTH, dtype=F32),
            buf(2, COLS, DEPTH, dtype=F32),
            pltpu.SemaphoreType.DMA,
            pltpu.SemaphoreType.DMA((copies,)),
            pltpu.SemaphoreType.DMA((copies,)),
        ],
        compiler_params=pltpu.CompilerParams(
            collective_id=0, has_side_effects=True, vmem_limit_bytes=56 * 2**20
        ),
        name="step",
    )(tower, cls_weight, box_weight, bias, labels, target_index, boxes)

    cls_grad, box_grad, bias_grad = pl.pallas_call(
        scale_kernel,
        out_shape=(
            jax.ShapeDtypeStruct((CLS, WIDTH), F32),
            jax.ShapeDtypeStruct((4 * ANCHORS, WIDTH), F32),
            jax.ShapeDtypeStruct((8, COLS), F32),
        ),
        in_specs=[vmem, vmem],
        out_specs=(pl.BlockSpec(memory_space=pl.ANY), vmem, vmem),
        scratch_shapes=[
            buf(4, BLOCK, WIDTH, dtype=F32),
            pltpu.SemaphoreType.DMA((4,)),
        ],
        compiler_params=pltpu.CompilerParams(vmem_limit_bytes=40 * 2**20),
        name="scale",
    )(r, s)
    flat = bias_grad.reshape(-1)
    loss = (s[6, 0] + s[6, 1]) / s[6, 2]
    return loss, cls_grad, flat[:CLS], box_grad, flat[CLS:OUTS], tower_grad


def solution(mesh):
    zl_count = mesh.shape["tile"] // (2 * RING)
    zh_count = mesh.shape["img"] // RING
    placed = (
        P("img", "tile", None, None),
        P(),
        P(),
        P(),
        P(),
        P("img", None, "tile", None),
        P("img", None, "tile", None),
        P("img", None, None),
    )
    return jax.shard_map(
        functools.partial(per_device, zl_count, zh_count),
        mesh=mesh,
        in_specs=placed,
        out_specs=(P(), P(), P(), P(), P(), P("img", "tile", None, None)),
        check_vma=False,
    )
```

time: 433 us -> 89.4 us (0.21)
  waiting for transfers between devices: 154 us -> 0 us
  local copies, waits for them, and re-layouts: 107 us -> 6.56 us
  blocking collectives: 83.6 us -> 0 us
  Pallas kernels: 0 us -> 78 us
  other arithmetic: 46 us -> 0.78 us
  between operations: 19 us -> 3.78 us
  starting transfers between devices: 12.1 us -> 0 us
  matrix products: 9.22 us -> 0 us
    psum x1 -> x0, waiting for transfers between devices: 154 us -> none  [per_device(): weight_sum = lax.psum(weight_terms, ('tile', 'img'))]
    psum x1 -> x0, blocking collectives: 83.6 us -> none  [packed_total(): subtotal = lax.psum(vector, axis)]
    pallas_call x0 -> x2, Pallas kernels: none -> 78 us  [the longest x1 73 us: per_device(): pl.pallas_call(functools.partial(step_kernel, zl_count, zh_count), out_sh...]
    gather x3 -> x0, local copies, waits for them, and re-layouts: 75 us -> none  [head_terms(): jnp.take_along_axis(boxes, jnp.broadcast_to(flat_index[:, None, :], (imag...]
    another operation x5 -> x0, other arithmetic: 14.9 us -> none
    ppermute x4 -> x0, starting transfers between devices: 12.1 us -> none  [the longest x2 7.71 us: padded_2(): before = lax.ppermute(last, axis, up)]
    scatter-add x7 -> x0, local copies, waits for them, and re-layouts: 11.1 us -> none  [taps_back(): accumulated = accumulated.at[:, row_tap:row_tap + rows_in, col_tap:col_ta...]
    dot_general x3 -> x0, matrix products: 9.22 us -> none  [the longest x1 4.04 us: per_device(): lax.dot_general(grad_rows.reshape(grad_rows.shape[0], -1), weight_all, ((...]
  transfers between devices with their start and end apart: 5 -> 0, of which waited for: 1 -> 0; matrix products, arithmetic and copies ran while one was open for 28% -> 0% of each run, Pallas kernels for 0% -> 0%
where the time goes in v1:
time: 89.4 us; the launch traced here: 89.1 us
  Pallas kernels  78 us (87%)
  local copies, waits for them, and re-layouts  6.56 us (7%)
  between operations  3.78 us (4%)
    pallas_call x1, Pallas kernels, per_device(): pl.pallas_call(functools.partial(step_kernel, zl_count, zh_count), out_sh...  73 us
    pallas_call x1, Pallas kernels, per_device(): pl.pallas_call(scale_kernel, out_shape=(jax.ShapeDtypeStruct((CLS, WIDTH)...  4.94 us
    unnamed x7, local copies, waits for them, and re-layouts  3.33 us

profile of v1, /device:TPU:1, one launch (start us, length us, event | category | flops | bytes accessed | tf_op | source)
XLA Modules:
  0.0 89.1 jit_solution(9274096113975014034)
XLA Ops:
  0.6 0.8 pad_maximum_fusion
  1.4 0.6 broadcast_in_dim.3.bias
  2.0 73.0 %step.1 = (bf16[2,4,4,48,1152]{4,3,2,1,0:T(8,128)(2,1)}, f32[8,128]{1,0:T(8,128)}, bf16[1,2,128,256]{3,2,1,0:T(8,128)(2,1)}) custom-call(bf16[1,2,128,256]{3,2,1,0:T(8,128)(2,1)} %tower.1, bf16[720,2304]{1,0:T(8,128)(2,1)} %wc_hbm.1, bf16[36,2304]{1,0:T(8,128)(2,1)} %wb.1, f32[1,768]{1,0:T(1,128)} %broadcast_in_dim.3.bias, s32[1,9,2,128]{3,2,1,0:T(2,128)} %labels.1, ...), custom_call_target="tpu_custom_call" | custom-call | tf_op jit(solution)/shard_map/step/pallas_call | solution.py:627
  75.1 1.4 %fusion = (f32[1,1]{1,0:T(1,128)}, f32[1,1]{1,0:T(1,128)}, f32[1,1]{1,0:T(1,128)}) fusion(f32[8,128]{1,0:T(8,128)} %get-tuple-element.12.s), kind=kLoop, calls=%fused_computation.1 | loop fusion | bytes 24 | tf_op jit(solution)/shard_map/slice | solution.py:704
  78.4 0.0 copy-start
  78.4 2.0 %copy-done = bf16[2,4,4,48,1152]{4,3,2,1,0:T(8,128)(2,1)S(1)} copy-done((bf16[2,4,4,48,1152]{4,3,2,1,0:T(8,128)(2,1)S(1)}, bf16[2,4,4,48,1152]{4,3,2,1,0:T(8,128)(2,1)}, u32[]{:S(2)}) %copy-start) | copy-done | bytes 3538968
  80.4 0.0 copy-start.1
  80.4 0.7 copy-done.1
  81.1 0.0 copy-start.2
  81.1 4.9 %scale.1 = (f32[720,2304]{1,0:T(8,128)}, f32[36,2304]{1,0:T(8,128)}, f32[8,128]{1,0:T(8,128)}) custom-call(bf16[2,4,4,48,1152]{4,3,2,1,0:T(8,128)(2,1)S(1)} %copy-done, f32[8,128]{1,0:T(8,128)S(1)} %copy-done.1), custom_call_target="tpu_custom_call" | custom-call | tf_op jit(solution)/shard_map/scale/pallas_call | solution.py:687
  86.1 1.3 %slice.19 = f32[36]{0:T(128)} slice(f32[1024]{0:T(1024)} %bitcast.3), slice={[720:756]} | slice | bytes 288 | tf_op jit(solution)/shard_map/slice | solution.py:705
  87.3 0.0 copy-done.2
  87.3 0.7 copy.15
  (1 shorter events, 0.0 us)
Async XLA Ops:
  78.4 2.0 %copy-start = (bf16[2,4,4,48,1152]{4,3,2,1,0:T(8,128)(2,1)S(1)}, bf16[2,4,4,48,1152]{4,3,2,1,0:T(8,128)(2,1)}, u32[]{:S(2)}) copy-start(bf16[2,4,4,48,1152]{4,3,2,1,0:T(8,128)(2,1)} %get-tuple-element.13.r) | copy-start | bytes 10616836
  80.4 0.7 copy-start.1
  81.1 6.2 %copy-start.2 = (bf16[1,2,128,256]{3,2,1,0:T(8,128)(2,1)S(1)}, bf16[1,2,128,256]{3,2,1,0:T(8,128)(2,1)}, u32[]{:S(2)}) copy-start(bf16[1,2,128,256]{3,2,1,0:T(8,128)(2,1)} %get-tuple-element.32) | copy-start | bytes 393220

commit v2 on v1

--- a/solution.py
+++ b/solution.py
@@ -126,12 +126,12 @@
 
 def step_kernel(
     zl_count, zh_count,
-    tower, wc_hbm, wb, bias, labels, tindex, boxes,
-    r_out, s_out, tg_out,
-    w, wbs, patches, halo, outs, gf, glow, boxy, acc, send_c, recv_c,
+    tower, wc_hbm, wb, cls_bias, box_bias, labels, tindex, boxes,
+    r_out, q_out, s_out, tg_out,
+    w, wbs, bias_row, patches, halo, outs, gf, glow, boxy, acc, send_c, recv_c,
     a1s, a1r, a2s, a2r, accb, b1s0, b1r0, b2s0, b2r0, b1s1, b1r1, b2s1, b2r1,
-    zf, zs, zr, zg, sc, sx, sy, sz, dpatch, edge_s, edge_r,
-    wsem, send, recv,
+    zf, zs, zr, zg, small, sz, dpatch, edge_s, edge_r,
+    wsem, ready, send, recv,
 ):
     t = lax.axis_index("tile")
     m = lax.axis_index("img")
@@ -168,11 +168,13 @@
         pl.semaphore_signal(barrier, inc=1, device_id=device, device_id_type=MESH)
 
     greet(sibling)
-    for k in range(1, RING):
-        greet(at((x + k) % RING, y, z, c))
-        greet(at(x, (y + k) % RING, z, c))
-    for k in range(1, nz):
-        greet(at(x, y, (z + k) % nz, c))
+    for near in (flip(a), 3 - a):
+        greet(ring(near, b))
+    for near in (flip(b), 3 - b):
+        greet(ring(a, near))
+    beside_z = (at(x, y, (z + 1) % nz, c), at(x, y, (z + nz - 1) % nz, c))
+    for device in beside_z:
+        greet(device)
 
     @pl.when(t > 0)
     def _():
@@ -208,11 +210,25 @@
     fill(tower[0, 0], 1)
     fill(tower[0, 1], 2)
 
-    greeted = 1 + 2 * (RING - 1) + nz - 1
+    greeted = 1 + 4 + 2
     pl.semaphore_wait(
         barrier, greeted + (t > 0).astype(jnp.int32) + (t < tiles - 1).astype(jnp.int32)
     )
 
+    rounds = nz // 2 - 1
+
+    def tell(k):
+        if k < rounds:
+            for device in beside_z:
+                pl.semaphore_signal(ready.at[k], inc=1, device_id=device, device_id_type=MESH)
+
+    def hear(k):
+        if k < rounds:
+            pl.semaphore_wait(ready.at[k], 2)
+            tell(k + 1)
+
+    tell(0)
+
     halo_up = links.make(tower.at[0, 0], halo.at[1], above)
     halo_down = links.make(tower.at[0, 1], halo.at[0], below)
 
@@ -232,7 +248,29 @@
     def _():
         halo[1] = jnp.zeros(halo.shape[1:], BF16)
 
+    nt = (((1,), (1,)), ((), ()))
+
+    def product(lhs, rhs):
+        return lax.dot_general(lhs, rhs, nt, preferred_element_type=F32)
+
+    def column(values):
+        wide = jnp.broadcast_to(values, (8, values.shape[1]))
+        return jnp.transpose(wide)[:, 0:1]
+
+    edge = 3 * DEPTH
+    patches[0, 0:COLS, 0:edge] = jnp.zeros((COLS, edge), BF16)
+    patches[1, COLS : 2 * COLS, HALF - edge : HALF] = jnp.zeros((COLS, edge), BF16)
+    bias_row[0:1, 0:CLS] = cls_bias[...].reshape(1, CLS)
+    bias_row[0:1, CLS:OUTS] = box_bias[...].reshape(1, OUTS - CLS)
+    bias_row[0:1, OUTS:PAD_OUTS] = jnp.zeros((1, PAD_OUTS - OUTS), F32)
+    bias_col = column(bias_row[0:1, :])
     load.wait()
+    for lhs, rows in ((w, slice(0, CLS)), (wbs, slice(CLS, PAD_OUTS))):
+        outs[rows, :] = (
+            product(lhs[:, 0:HALF], patches[0])
+            + product(lhs[:, HALF:WIDTH], patches[1])
+            + bias_col[rows]
+        )
 
     @pl.when(t < tiles - 1)
     def _():
@@ -244,21 +282,12 @@
 
     fill(halo[0], 0)
     fill(halo[1], 3)
-
-    nt = (((1,), (1,)), ((), ()))
-
-    def product(lhs, rhs):
-        return lax.dot_general(lhs, rhs, nt, preferred_element_type=F32)
-
-    bias_col = jnp.transpose(jnp.broadcast_to(bias[...], (8, PAD_OUTS)))[:, 0:1]
-    outs[0:CLS, :] = (
-        product(w[:, 0:HALF], patches[0]) + product(w[:, HALF:WIDTH], patches[1]) + bias_col[0:CLS]
-    )
-    outs[CLS:PAD_OUTS, :] = (
-        product(wbs[:, 0:HALF], patches[0])
-        + product(wbs[:, HALF:WIDTH], patches[1])
-        + bias_col[CLS:PAD_OUTS]
-    )
+    for lhs, rows in ((w, slice(0, CLS)), (wbs, slice(CLS, PAD_OUTS))):
+        outs[rows, 0:COLS] += product(lhs[:, 0:edge], patches[0, 0:COLS, 0:edge])
+        outs[rows, COLS : 2 * COLS] += product(
+            lhs[:, WIDTH - edge : WIDTH], patches[1, COLS : 2 * COLS, HALF - edge : HALF]
+        )
+    hear(0)
 
     class_ids = lax.broadcasted_iota(jnp.int32, (CLASSES, COLS), 0)
 
@@ -304,12 +333,45 @@
         gf[CLS:PAD_OUTS, lanes] = boxy[here]
     glow[CLS:PAD_OUTS, :] = gf[CLS:PAD_OUTS, :].astype(BF16)
 
+    hear(1)
+
     send_to_core = []
     for k in range(RING):
         rows = slice(k * RING * BLOCK, (k + 1) * RING * BLOCK)
         part = jnp.dot(glow[rows, :], patches[1 - c], preferred_element_type=F32)
         send_c[k] = part.astype(BF16).reshape(RING, BLOCK, HALF)
         send_to_core.append(links.push(send_c.at[k], recv_c.at[k], sibling))
+
+    def own(k, carry):
+        rows = pl.ds(pl.multiple_of(k * RING * BLOCK, RING * BLOCK), RING * BLOCK)
+        part = jnp.dot(glow[rows, :], patches[c], preferred_element_type=F32)
+        acc[k] = part.reshape(RING, BLOCK, HALF)
+        return carry
+
+    lax.fori_loop(0, RING, own, 0)
+
+    hear(2)
+    for copy in send_to_core:
+        copy.wait_recv()
+
+    def pair(quarter, j):
+        return acc[quarter, j] + recv_c[quarter, j].astype(F32)
+
+    steps_a = ((flip(a), 3 - a), (3 - a, flip(a)))
+    first = {}
+    for which in (1, 0):
+        for s in range(2):
+            near, far = steps_a[s]
+            back = (3 - near, flip(near))[s]
+            quarter = back if which else near
+            for j in range(2):
+                a1s[s, which, j] = pair(quarter, 2 * s + j).astype(BF16)
+            first[s, which] = links.push(a1s.at[s, which], a1r.at[s, which], ring(near, b))
+
+    tn = (((0,), (0,)), ((), ()))
+    dpatch[...] = lax.dot_general(
+        glow[0:CLS, :], w[...], tn, preferred_element_type=F32
+    ) + lax.dot_general(glow[CLS:PAD_OUTS, :], wbs[...], tn, preferred_element_type=F32)
 
     sums = lax.dot_general(
         jnp.ones((8, 2 * COLS), F32), gf[...], nt,
@@ -323,43 +385,20 @@
     scalars = (jnp.sum(focal_sum), jnp.sum(giou), jnp.sum(positive))
     for k, value in enumerate(scalars):
         mine = jnp.where((rows8 == 6) & (lane == k), value, mine)
-    sc[c] = mine
-    small_c = links.push(sc.at[c], sc.at[c], sibling)
-
-    def own(k, carry):
-        rows = pl.ds(pl.multiple_of(k * RING * BLOCK, RING * BLOCK), RING * BLOCK)
-        part = jnp.dot(glow[rows, :], patches[c], preferred_element_type=F32)
-        acc[k] = part.reshape(RING, BLOCK, HALF)
-        return carry
-
-    lax.fori_loop(0, RING, own, 0)
-
-    small_c.wait_recv()
-    sx[x] = sc[0] + sc[1]
-    small_x = [
-        links.push(sx.at[x], sx.at[x], at((x + k) % RING, y, z, c)) for k in range(1, RING)
-    ]
-    for copy in send_to_core:
-        copy.wait_recv()
-
-    def pair(quarter, j):
-        return acc[quarter, j] + recv_c[quarter, j].astype(F32)
-
-    steps_a = ((flip(a), 3 - a), (3 - a, flip(a)))
-    first = {}
-    for which in (1, 0):
-        for s in range(2):
-            near, far = steps_a[s]
-            back = (3 - near, flip(near))[s]
-            quarter = back if which else near
-            for j in range(2):
-                a1s[s, which, j] = pair(quarter, 2 * s + j).astype(BF16)
-            first[s, which] = links.push(a1s.at[s, which], a1r.at[s, which], ring(near, b))
-
-    tn = (((0,), (0,)), ((), ()))
-    dpatch[...] = lax.dot_general(
-        glow[0:CLS, :], w[...], tn, preferred_element_type=F32
-    ) + lax.dot_general(glow[CLS:PAD_OUTS, :], wbs[...], tn, preferred_element_type=F32)
+    stages = (sibling,) + tuple(ring(n, b) for n in (flip(a), 3 - a)) + tuple(
+        ring(a, n) for n in (flip(b), 3 - b)
+    )
+    doubling = []
+
+    def double(k):
+        if k == 0:
+            small[0, 0] = mine
+        else:
+            doubling[k - 1].wait_recv()
+            small[k, 0] = small[k - 1, 0] + small[k - 1, 1]
+        doubling.append(links.push(small.at[k, 0], small.at[k, 1], stages[k]))
+
+    double(0)
 
     def reach(row_tap, here):
         total = None
@@ -398,12 +437,7 @@
             a2s[s, j] = (pair(far, 2 * s + j) + a1r[s, 1, j].astype(F32)).astype(BF16)
         second.append(links.push(a2s.at[s], a2r.at[s], ring(far, b)))
 
-    for copy in small_x:
-        copy.wait_recv()
-    sy[y] = (sx[0] + sx[1]) + (sx[2] + sx[3])
-    small_y = [
-        links.push(sy.at[y], sy.at[y], at(x, (y + k) % RING, z, c)) for k in range(1, RING)
-    ]
+    double(1)
 
     tg_own = (reach(1, 0) + reach(0, 1), reach(2, 0) + reach(1, 1))
 
@@ -425,6 +459,8 @@
             accb[2 * s + j] = (
                 pair(a, 2 * s + j) + a1r[s, 0, j].astype(F32) + a2r[s, j].astype(F32)
             )
+
+    double(2)
 
     steps_b = ((flip(b), 3 - b), (3 - b, flip(b)))
     bufs = ((b1s0, b1r0, b2s0, b2r0, slice(0, SPLIT)), (b1s1, b1r1, b2s1, b2r1, slice(SPLIT, HALF)))
@@ -444,12 +480,7 @@
         first[s, 1].wait_recv()
         s2[...] = (accb[far, :, cols] + r1[1].astype(F32)).astype(BF16)
         second.append(links.push(s2, r2, ring(a, far)))
-    for copy in small_y:
-        copy.wait_recv()
-    sz[z] = (sy[0] + sy[1]) + (sy[2] + sy[3])
-    small_z = [
-        links.push(sz.at[z], sz.at[z], at(x, y, (z + k) % nz, c)) for k in range(1, nz)
-    ]
+    double(3)
     per = zf.shape[1] // 8
     groups = BLOCK // 8
     zf[...] = jnp.zeros(zf.shape, F32)
@@ -470,6 +501,7 @@
     turns = [
         links.push(zs.at[(z + k) % nz], zr.at[z], at(x, y, (z + k) % nz, c)) for k in range(1, nz)
     ]
+    double(4)
     total = zf[z]
     for k in range(1, nz):
         turns[k - 1].wait_recv()
@@ -477,6 +509,11 @@
     zg[z] = total.astype(BF16)
     turns = [
         links.push(zg.at[z], zg.at[z], at(x, y, (z + k) % nz, c)) for k in range(1, nz)
+    ]
+    doubling[4].wait_recv()
+    sz[z] = small[4, 0] + small[4, 1]
+    small_z = [
+        links.push(sz.at[z], sz.at[z], at(x, y, (z + k) % nz, c)) for k in range(1, nz)
     ]
     for copy in turns:
         copy.wait_recv()
@@ -494,8 +531,17 @@
     top, bottom = slice(0, 32), slice(32, BLOCK)
     shared = []
 
+    def square(h, a_, b_):
+        value = r_out[h, a_, b_].astype(F32)
+        value = jnp.sum((value * value).reshape(BLOCK // 8, 8, HALF), axis=0)
+        total = value[:, 0:COLS]
+        for j in range(1, HALF // COLS):
+            total = total + value[:, j * COLS : (j + 1) * COLS]
+        q_out[h, a_, b_] = total
+
     def share(a_, b_):
         shared.append(links.push(r_out.at[c, a_, b_], r_out.at[c, a_, b_], sibling))
+        square(c, a_, b_)
 
     def along_a(b_):
         block = r_out.at[c, a, b_]
@@ -550,6 +596,12 @@
 
     for copy in shared:
         copy.wait_recv()
+
+    def other(k, carry):
+        square(1 - c, k // RING, k % RING)
+        return carry
+
+    lax.fori_loop(0, RING * RING, other, 0)
     links.drain()
 
     @pl.when(t > 0)
@@ -563,24 +615,23 @@
         edge_down.wait_send()
 
 
-def scale_kernel(r, s, cls_out, box_out, bias_out, stage, sem):
-    def squares(k, total):
-        for h in range(2):
-            value = r[h, k // RING, k % RING].astype(F32)
-            value = value * value
-            value = jnp.sum(value.reshape(BLOCK // 8, 8, HALF), axis=0)
-            for j in range(HALF // COLS):
-                total = total + value[:, j * COLS : (j + 1) * COLS]
-        return total
-
-    total = lax.fori_loop(0, RING * RING, squares, jnp.zeros((8, COLS), F32))
+def scale_kernel(r, q, s, tg, cls_out, box_out, loss_out, cls_bias_out, box_bias_out, tg_out, stage, sem):
+    slots = stage.shape[0]
+    tower_copy = pltpu.make_async_copy(tg, tg_out, sem.at[slots])
+    tower_copy.start()
     rows8 = lax.broadcasted_iota(jnp.int32, (8, COLS), 0)
     bias = jnp.where(rows8 < PAD_OUTS // COLS, s[...], 0.0)
-    total = jnp.sum(total + bias * bias, keepdims=True)
+    total = bias * bias
+    for k in range(2 * RING * RING):
+        total = total + q[k // (RING * RING), k // RING % RING, k % RING]
+    total = jnp.sum(total, keepdims=True)
     scale = lax.rsqrt(total / (OUTS * (WIDTH + 1)) + NORM_EPS)
-    bias_out[...] = bias * scale
-
-    slots = stage.shape[0]
+    bias = bias * scale
+    cls_bias_out[...] = bias
+    at_row, at_lane = CLS // COLS, CLS % COLS
+    box_bias_out[...] = pltpu.roll(bias, COLS - at_lane, 1)[at_row : at_row + 1]
+    loss_out[...] = (s[6:7, 0:1] + s[6:7, 1:2]) / s[6:7, 2:3]
+
     count = CLS // BLOCK
 
     def store(k):
@@ -609,6 +660,7 @@
         )[0 : 4 * ANCHORS]
     for k in range(count - slots, count):
         store(k).wait()
+    tower_copy.wait()
 
 
 def per_device(
@@ -617,30 +669,31 @@
     nz = zl_count * zh_count
     tiles8 = BLOCK // 8 * (HALF // COLS)
     per = -(-tiles8 // nz) * 8
-    bias = jnp.concatenate([cls_bias, box_bias, jnp.zeros((PAD_OUTS - OUTS,), F32)])[None]
     vmem = pl.BlockSpec(memory_space=pltpu.VMEM)
     copies = 100 + 4 * nz
 
     def buf(*shape, dtype=BF16):
         return pltpu.VMEM(shape, dtype)
 
-    r, s, tower_grad = pl.pallas_call(
+    r, q, s, tower_grad = pl.pallas_call(
         functools.partial(step_kernel, zl_count, zh_count),
         out_shape=(
-            jax.ShapeDtypeStruct((2, RING, RING, BLOCK, HALF), BF16),
-            jax.ShapeDtypeStruct((8, COLS), F32),
-            jax.ShapeDtypeStruct(tower.shape, BF16),
+            buf(2, RING, RING, BLOCK, HALF),
+            buf(2, RING, RING, 8, COLS, dtype=F32),
+            buf(8, COLS, dtype=F32),
+            buf(*tower.shape),
         ),
         in_specs=[
             vmem,
             pl.BlockSpec(memory_space=pl.ANY),
-            vmem, vmem, vmem, vmem,
+            vmem, vmem, vmem, vmem, vmem,
             pl.BlockSpec(memory_space=pltpu.SMEM),
         ],
-        out_specs=(vmem, vmem, vmem),
+        out_specs=(vmem, vmem, vmem, vmem),
         scratch_shapes=[
             buf(CLS, WIDTH),
             buf(PAD_OUTS - CLS, WIDTH),
+            buf(8, PAD_OUTS, dtype=F32),
             buf(2, 2 * COLS, HALF),
             buf(2, COLS, DEPTH),
             buf(PAD_OUTS, 2 * COLS, dtype=F32),
@@ -667,14 +720,13 @@
             buf(nz, per, COLS),
             buf(nz, per, COLS),
             buf(nz, per, COLS),
-            buf(2, 8, COLS, dtype=F32),
-            buf(RING, 8, COLS, dtype=F32),
-            buf(RING, 8, COLS, dtype=F32),
+            buf(5, 2, 8, COLS, dtype=F32),
             buf(nz, 8, COLS, dtype=F32),
             buf(2 * COLS, WIDTH, dtype=F32),
             buf(2, COLS, DEPTH, dtype=F32),
             buf(2, COLS, DEPTH, dtype=F32),
             pltpu.SemaphoreType.DMA,
+            pltpu.SemaphoreType.REGULAR((max(nz // 2 - 1, 1),)),
             pltpu.SemaphoreType.DMA((copies,)),
             pltpu.SemaphoreType.DMA((copies,)),
         ],
@@ -682,27 +734,36 @@
             collective_id=0, has_side_effects=True, vmem_limit_bytes=56 * 2**20
         ),
         name="step",
-    )(tower, cls_weight, box_weight, bias, labels, target_index, boxes)
-
-    cls_grad, box_grad, bias_grad = pl.pallas_call(
+    )(tower, cls_weight, box_weight, cls_bias, box_bias, labels, target_index, boxes)
+
+    hbm = pl.BlockSpec(memory_space=pl.ANY)
+    cls_grad, box_grad, loss, cls_bias_grad, box_bias_grad, tower_grad = pl.pallas_call(
         scale_kernel,
         out_shape=(
             jax.ShapeDtypeStruct((CLS, WIDTH), F32),
-            jax.ShapeDtypeStruct((4 * ANCHORS, WIDTH), F32),
+            jax.ShapeDtypeStruct((OUTS - CLS, WIDTH), F32),
+            jax.ShapeDtypeStruct((1, 1), F32),
             jax.ShapeDtypeStruct((8, COLS), F32),
+            jax.ShapeDtypeStruct((1, COLS), F32),
+            jax.ShapeDtypeStruct(tower.shape, BF16),
         ),
-        in_specs=[vmem, vmem],
-        out_specs=(pl.BlockSpec(memory_space=pl.ANY), vmem, vmem),
+        in_specs=[vmem, vmem, vmem, vmem],
+        out_specs=(hbm, vmem, vmem, vmem, vmem, hbm),
         scratch_shapes=[
             buf(4, BLOCK, WIDTH, dtype=F32),
-            pltpu.SemaphoreType.DMA((4,)),
+            pltpu.SemaphoreType.DMA((5,)),
         ],
         compiler_params=pltpu.CompilerParams(vmem_limit_bytes=40 * 2**20),
         name="scale",
-    )(r, s)
-    flat = bias_grad.reshape(-1)
-    loss = (s[6, 0] + s[6, 1]) / s[6, 2]
-    return loss, cls_grad, flat[:CLS], box_grad, flat[CLS:OUTS], tower_grad
+    )(r, q, s, tower_grad)
+    return (
+        loss.reshape(()),
+        cls_grad,
+        cls_bias_grad.reshape(-1)[:CLS],
+        box_grad,
+        box_bias_grad.reshape(-1)[: OUTS - CLS],
+        tower_grad,
+    )
 
 
 def solution(mesh):

time: 89.4 us -> 75.4 us (0.84)
  local copies, waits for them, and re-layouts: 6.56 us -> 0.51 us
  Pallas kernels: 78 us -> 74.1 us
  between operations: 3.78 us -> 0.65 us
    pallas_call x1, Pallas kernels: 73 us -> 69.6 us  [per_device(): pl.pallas_call(functools.partial(step_kernel, zl_count, zh_count), out_sh...]
    unnamed x7 -> x0, local copies, waits for them, and re-layouts: 3.33 us -> none
    slice x2 -> x1, local copies, waits for them, and re-layouts: 2.65 us -> 0.51 us  [per_device(): box_bias_grad.reshape(-1)[:OUTS - CLS]]
where the time goes in v2:
time: 75.4 us; the launch traced here: 75.2 us
  Pallas kernels  74.1 us (98%)
    pallas_call x1, Pallas kernels, per_device(): pl.pallas_call(functools.partial(step_kernel, zl_count, zh_count), out_sh...  69.6 us
    pallas_call x1, Pallas kernels, per_device(): pl.pallas_call(scale_kernel, out_shape=(jax.ShapeDtypeStruct((CLS, WIDTH)...  4.47 us

profile of v2, /device:TPU:1, one launch (start us, length us, event | category | flops | bytes accessed | tf_op | source)
XLA Modules:
  0.0 75.2 jit_solution(9699313708285812050)
XLA Ops:
  0.6 69.6 %step.1 = (bf16[2,4,4,48,1152]{4,3,2,1,0:T(8,128)(2,1)S(1)}, f32[2,4,4,8,128]{4,3,2,1,0:T(8,128)S(1)}, f32[8,128]{1,0:T(8,128)S(1)}, bf16[1,2,128,256]{3,2,1,0:T(8,128)(2,1)S(1)}) custom-call(bf16[1,2,128,256]{3,2,1,0:T(8,128)(2,1)} %tower.1, bf16[720,2304]{1,0:T(8,128)(2,1)} %wc_hbm.1, bf16[36,2304]{1,0:T(8,128)(2,1)} %wb.1, f32[720]{0:T(1024)} %cls_bias.1, ...), custom_call_target="tpu_custom_call" | custom-call | tf_op jit(solution)/shard_map/step/pallas_call | solution.py:678
  70.2 4.5 %scale.1 = (f32[720,2304]{1,0:T(8,128)}, f32[36,2304]{1,0:T(8,128)}, f32[1,1]{1,0:T(1,128)}, f32[8,128]{1,0:T(8,128)}, f32[1,128]{1,0:T(1,128)S(1)}, /*index=5*/bf16[1,2,128,256]{3,2,1,0:T(8,128)(2,1)}) custom-call(bf16[2,4,4,48,1152]{4,3,2,1,0:T(8,128)(2,1)S(1)} %get-tuple-element.16.r, f32[2,4,4,8,128]{4,3,2,1,0:T(8,128)S(1)} %get-tuple-element.17.q, ...), custom_call_target="tpu_custom_call" | custom-call | tf_op jit(solution)/shard_map/scale/pallas_call | solution.py:740
  74.7 0.5 slice_bitcast_fusion

commit v3 on v2

v3 whole, which is shorter than its diff:
```python
import functools

import jax
import jax.numpy as jnp
import numpy as np
from jax import lax
from jax.experimental import pallas as pl
from jax.experimental.pallas import tpu as pltpu
from jax.sharding import PartitionSpec as P

CLASSES = 80
ANCHORS = 9
STRIDE = 8
FOCAL_ALPHA = 0.25
NORM_EPS = 1e-06

RING = 4
IN_FLIGHT = 40
RECEIVES = 74
GROUPS = 9
CLS = ANCHORS * CLASSES
OUTS = CLS + 4 * ANCHORS
PAD_OUTS = 768
TAPS = 9
DEPTH = 256
WIDTH = TAPS * DEPTH
HALF = WIDTH // 2
COLS = 128
BLOCK = PAD_OUTS // (RING * RING)
STREAMS = ((0, 640, 384), (640, 1152, 256))
BF16 = jnp.bfloat16
F32 = jnp.float32
MESH = pl.DeviceIdType.MESH


def flip(i):
    return i + 1 - 2 * (i % 2)


class Links:
    def __init__(self, send, recv):
        self.send, self.recv = send, recv
        self.sends = self.recvs = 0
        self.sent, self.groups = [], []

    def make(self, src, dst, device, pair=None):
        send_id, recv_id = self.pair() if pair is None else pair
        return pltpu.make_async_remote_copy(
            src_ref=src,
            dst_ref=dst,
            send_sem=self.send.at[send_id],
            recv_sem=self.recv.at[recv_id],
            device_id=device,
            device_id_type=MESH,
        )

    def pair(self):
        self.sends += 1
        self.recvs += 1
        return IN_FLIGHT + self.sends - 1, self.recvs - 1

    def push(self, src, dst, device):
        slot = len(self.sent) % IN_FLIGHT
        if len(self.sent) >= IN_FLIGHT:
            self.sent[-IN_FLIGHT].wait_send()
        self.recvs += 1
        copy = self.make(src, dst, device, (slot, self.recvs - 1))
        copy.start()
        self.sent.append(copy)
        return copy

    def group(self, whole, device):
        pair = self.pair()
        both = self.make(whole, whole, device, pair)
        self.groups.append(both)

        def start(src, dst, to):
            self.make(src, dst, to, pair).start()

        return start, both.wait_recv

    def drain(self):
        for copy in self.sent[-IN_FLIGHT:]:
            copy.wait_send()
        for both in self.groups:
            both.wait_send()


def anchor_sizes():
    ids = np.arange(ANCHORS)
    base = np.float32(4.0 * STRIDE) * np.exp2((ids // 3).astype(np.float32) / np.float32(3.0))
    ratio = (ids % 3 - 1).astype(np.float32) / np.float32(2.0)
    return (base * np.exp2(-ratio)).astype(np.float32), (base * np.exp2(ratio)).astype(np.float32)


def box_terms(offsets, assigned, corners, first_row):
    shape = assigned.shape
    ids = lax.broadcasted_iota(jnp.int32, shape, 0)
    lanes = lax.broadcasted_iota(jnp.int32, shape, 1)
    widths, heights = anchor_sizes()
    anchor_w = jnp.zeros(shape, F32)
    anchor_h = jnp.zeros(shape, F32)
    for a in range(ANCHORS):
        anchor_w = jnp.where(ids == a, float(widths[a]), anchor_w)
        anchor_h = jnp.where(ids == a, float(heights[a]), anchor_h)
    second = (lanes >= COLS).astype(jnp.int32)
    centre_y = ((first_row + second).astype(F32) + 0.5) * STRIDE
    centre_x = ((lanes - COLS * second).astype(F32) + 0.5) * STRIDE
    true_left, true_top, true_right, true_bottom = corners
    positive = (assigned >= 0).astype(F32)

    def each(o0, o1, o2, o3):
        middle_x = centre_x + o0 * anchor_w
        middle_y = centre_y + o1 * anchor_h
        pred_width = anchor_w * jnp.exp(o2)
        pred_height = anchor_h * jnp.exp(o3)
        pred_left = middle_x - 0.5 * pred_width
        pred_right = middle_x + 0.5 * pred_width
        pred_top = middle_y - 0.5 * pred_height
        pred_bottom = middle_y + 0.5 * pred_height
        crossing_w = jnp.maximum(
            jnp.minimum(pred_right, true_right) - jnp.maximum(pred_left, true_left), 0.0
        )
        crossing_h = jnp.maximum(
            jnp.minimum(pred_bottom, true_bottom) - jnp.maximum(pred_top, true_top), 0.0
        )
        crossing = crossing_w * crossing_h
        union_area = (
            pred_width * pred_height
            + (true_right - true_left) * (true_bottom - true_top)
            - crossing
        )
        outer_w = jnp.maximum(pred_right, true_right) - jnp.minimum(pred_left, true_left)
        outer_h = jnp.maximum(pred_bottom, true_bottom) - jnp.minimum(pred_top, true_top)
        outer_area = outer_w * outer_h
        giou_value = crossing / union_area - (outer_area - union_area) / outer_area
        return positive * (1.0 - giou_value)

    values, pullback = jax.vjp(each, *offsets)
    return values, pullback(jnp.ones(shape, F32)), positive


def shifted(value, tap):
    if tap == 1:
        return value
    rows = lax.broadcasted_iota(jnp.int32, value.shape, 0)
    if tap == 0:
        return jnp.where(rows == 0, 0.0, pltpu.roll(value, 1, 0))
    return jnp.where(rows == COLS - 1, 0.0, pltpu.roll(value, COLS - 1, 0))


def step_kernel(
    zl_count, zh_count,
    tower, wc_hbm, wb, cls_bias, box_bias, labels, tindex, boxes,
    r_out0, r_out1, q_out, s_out, tg_out,
    w, wbs, bias_row, ext, patches, beside, outs, gf, glow, theirs, boxy,
    small, sz, dpatch, edge_s, edge_r,
    wsem, ready, send, recv, *per_stream,
):
    t = lax.axis_index("tile")
    m = lax.axis_index("img")
    tiles = zl_count * RING * 2
    nz = zl_count * zh_count
    c = t % 2
    y = (t // 2) % RING
    x = m // zh_count
    z = (m % zh_count) * zl_count + t // (2 * RING)

    def at(x_, y_, z_, c_):
        return {
            "tile": (z_ % zl_count) * (2 * RING) + y_ * 2 + c_,
            "img": x_ * zh_count + z_ // zl_count,
        }

    a = x + c * (y - x)
    b = y + c * (x - y)

    def ring(a_, b_):
        return at(a_ + c * (b_ - a_), b_ + c * (a_ - b_), z, c)

    sibling = at(x, y, z, 1 - c)
    outer = {"tile": t + 2 * c - 1, "img": m}
    has_outer = jnp.where(c == 0, t > 0, t < tiles - 1)
    links = Links(send, recv)

    load = pltpu.make_async_copy(wc_hbm, w, wsem)
    load.start()

    barrier = pltpu.get_barrier_semaphore()

    def greet(device):
        pl.semaphore_signal(barrier, inc=1, device_id=device, device_id_type=MESH)

    greet(sibling)
    for near in (flip(a), 3 - a):
        greet(ring(near, b))
    for near in (flip(b), 3 - b):
        greet(ring(a, near))
    beside_z = (at(x, y, (z + 1) % nz, c), at(x, y, (z + nz - 1) % nz, c))
    for device in beside_z:
        greet(device)

    @pl.when(has_outer)
    def _():
        greet(outer)

    wanted = jnp.concatenate([tindex[0, :, 0, :], tindex[0, :, 1, :]], axis=1)

    def pick(n, found):
        hit = wanted == n
        return tuple(jnp.where(hit, boxes[0, j, n], found[j]) for j in range(4))

    zero = jnp.zeros(wanted.shape, F32)
    corners = lax.fori_loop(0, boxes.shape[2], pick, (zero, zero, zero, zero))
    wbs[...] = jnp.zeros(wbs.shape, BF16)
    wbs[0 : 4 * ANCHORS, :] = wb[...]

    def fill(row, place, halves, put):
        value = row.astype(F32)
        for col_tap in range(3):
            piece = shifted(value, col_tap).astype(BF16)
            for here in range(2):
                row_tap = place - here
                if 0 <= row_tap <= 2:
                    for part in range(2):
                        k = (3 * row_tap + col_tap) * DEPTH + part * COLS
                        if k // HALF in halves:
                            put(
                                k // HALF,
                                slice(here * COLS, (here + 1) * COLS),
                                slice(k % HALF, k % HALF + COLS),
                                piece[:, part * COLS : (part + 1) * COLS],
                            )

    def put_own(half, rows, cols, value):
        patches[half, rows, cols] = value

    def put_beside(half, rows, cols, value):
        beside[rows, cols] = value

    for here in range(2):
        ext[1 + 2 * c + here] = tower[0, here]
        fill(tower[0, here], 1 + here, (0, 1), put_own)

    pl.semaphore_wait(barrier, 1 + 4 + 2 + has_outer.astype(jnp.int32))

    rounds = nz // 2 - 1

    def tell(k):
        if k < rounds:
            for device in beside_z:
                pl.semaphore_signal(ready.at[k], inc=1, device_id=device, device_id_type=MESH)

    def hear(k):
        if k < rounds:
            pl.semaphore_wait(ready.at[k], 2)
            tell(k + 1)

    halo = links.make(tower.at[0, c], ext.at[5 * (1 - c)], outer)

    @pl.when(has_outer)
    def _():
        halo.start()

    @pl.when(jnp.logical_not(has_outer))
    def _():
        ext[5 * c] = jnp.zeros(ext.shape[1:], BF16)

    rows_across = links.push(tower.at[0], ext.at[pl.ds(1 + 2 * c, 2)], sibling)
    tell(0)

    nt = (((1,), (1,)), ((), ()))

    def product(lhs, rhs):
        return lax.dot_general(lhs, rhs, nt, preferred_element_type=F32)

    def column(values):
        wide = jnp.broadcast_to(values, (8, values.shape[1]))
        return jnp.transpose(wide)[:, 0:1]

    edge = 3 * DEPTH
    patches[0, 0:COLS, 0:edge] = jnp.zeros((COLS, edge), BF16)
    patches[1, COLS : 2 * COLS, HALF - edge : HALF] = jnp.zeros((COLS, edge), BF16)
    bias_row[0:1, 0:CLS] = cls_bias[...].reshape(1, CLS)
    bias_row[0:1, CLS:OUTS] = box_bias[...].reshape(1, OUTS - CLS)
    bias_row[0:1, OUTS:PAD_OUTS] = jnp.zeros((1, PAD_OUTS - OUTS), F32)
    bias_col = column(bias_row[0:1, :])
    load.wait()
    for lhs, rows in ((w, slice(0, CLS)), (wbs, slice(CLS, PAD_OUTS))):
        outs[rows, :] = (
            product(lhs[:, 0:HALF], patches[0])
            + product(lhs[:, HALF:WIDTH], patches[1])
            + bias_col[rows]
        )

    rows_across.wait_recv()

    @pl.when(has_outer)
    def _():
        halo.wait_recv()

    outer_across = links.push(ext.at[5 * c], ext.at[5 * c], sibling)
    fill(ext[2 * c], 0, (0, 1), put_own)
    fill(ext[2 * c + 3], 3, (0, 1), put_own)
    for lhs, rows in ((w, slice(0, CLS)), (wbs, slice(CLS, PAD_OUTS))):
        outs[rows, 0:COLS] += product(lhs[:, 0:edge], patches[0, 0:COLS, 0:edge])
        outs[rows, COLS : 2 * COLS] += product(
            lhs[:, WIDTH - edge : WIDTH], patches[1, COLS : 2 * COLS, HALF - edge : HALF]
        )
    hear(0)

    class_ids = lax.broadcasted_iota(jnp.int32, (CLASSES, COLS), 0)

    def focal(anchor, total):
        rows = pl.ds(pl.multiple_of(anchor * CLASSES, CLASSES), CLASSES)
        for here in range(2):
            lanes = slice(here * COLS, (here + 1) * COLS)
            score = outs[rows, lanes]
            label = labels[0, anchor, here : here + 1, :]
            hit = jnp.broadcast_to(label, (CLASSES, COLS)) == class_ids
            counted = (label >= -1).astype(F32)
            side = jnp.where(hit, score, -score)
            small_e = jnp.exp(-jnp.abs(score))
            inverse = 1.0 / (1.0 + small_e)
            log_p = jnp.minimum(side, 0.0) - jnp.log1p(small_e)
            right = side >= 0
            p = jnp.where(right, inverse, small_e * inverse)
            miss = jnp.where(right, small_e * inverse, inverse)
            alpha = jnp.where(hit, FOCAL_ALPHA, FOCAL_ALPHA - 1.0) * counted
            weight = alpha * miss * miss
            grad = weight * (2.0 * p * log_p - miss)
            value = -jnp.abs(weight) * log_p
            gf[rows, lanes] = grad
            glow[rows, lanes] = grad.astype(BF16)
            total = total + jnp.sum(value.reshape(CLASSES // 8, 8, COLS), axis=0)
        return total

    focal_sum = lax.fori_loop(0, ANCHORS, focal, jnp.zeros((8, COLS), F32))

    assigned = jnp.concatenate([labels[0, :, 0, :], labels[0, :, 1, :]], axis=1)
    for here in range(2):
        boxy[here] = outs[CLS:PAD_OUTS, here * COLS : (here + 1) * COLS]
    offsets = [
        jnp.concatenate([boxy[here, pl.ds(j, ANCHORS, stride=4), :] for here in range(2)], axis=1)
        for j in range(4)
    ]
    giou, offset_grads, positive = box_terms(offsets, assigned, corners, 2 * t)
    boxy[...] = jnp.zeros(boxy.shape, F32)
    for here in range(2):
        lanes = slice(here * COLS, (here + 1) * COLS)
        for j in range(4):
            boxy[here, pl.ds(j, ANCHORS, stride=4), :] = offset_grads[j][:, lanes]
        gf[CLS:PAD_OUTS, lanes] = boxy[here]
    glow[CLS:PAD_OUTS, :] = gf[CLS:PAD_OUTS, :].astype(BF16)
    glow_across = links.push(glow, theirs, sibling)

    streams = []
    each = len(per_stream) // len(STREAMS)
    for k, (start, stop, cut) in enumerate(STREAMS):
        streams.append(((r_out0, r_out1)[k], start, stop, cut, *per_stream[k * each : (k + 1) * each]))
    for _, start, stop, _, acc, *_ in streams:
        part = jnp.dot(glow[...], patches[c, :, start:stop], preferred_element_type=F32)
        acc[...] = part.reshape(acc.shape)
    hear(1)
    outer_across.wait_recv()
    for half in range(2):

        @pl.when(c == half)
        def _():
            for place in range(4):
                fill(ext[2 * (1 - half) + place], place, (half,), put_beside)

    glow_across.wait_recv()

    def wrap(i):
        return (i + RING) % RING

    top, bottom = slice(0, 32), slice(32, BLOCK)
    groups = BLOCK // 8
    shared = []

    def square(k, h, a_, b_):
        r = streams[k][0]
        value = r[h, a_, b_].astype(F32)
        value = jnp.sum((value * value).reshape(groups, 8, value.shape[1]), axis=0)
        total = value[:, 0:COLS]
        for j in range(1, value.shape[1] // COLS):
            total = total + value[:, j * COLS : (j + 1) * COLS]
        q_out[k, h, a_, b_] = total

    def stream(
        number, r, start, stop, cut,
        acc, a1s, a1r, a2s, a2r, accb, b1s0, b1r0, b2s0, b2r0, b1s1, b1r1, b2s1, b2r1,
        zf, zs, zr, zg,
    ):
        width = stop - start
        part = jnp.dot(theirs[...], beside[:, start:stop], preferred_element_type=F32)
        acc[...] += part.reshape(acc.shape)

        steps = ((flip(a), 3 - a), (3 - a, flip(a)))
        first = {}
        for which in (1, 0):
            for s in range(2):
                near, far = steps[s]
                back = (3 - near, flip(near))[s]
                quarter = back if which else near
                for j in range(2):
                    a1s[s, which, j] = acc[quarter, 2 * s + j].astype(BF16)
                first[s, which] = links.push(a1s.at[s, which], a1r.at[s, which], ring(near, b))
        yield

        second = []
        for s in range(2):
            near, far = steps[s]
            first[s, 1].wait_recv()
            for j in range(2):
                a2s[s, j] = (acc[far, 2 * s + j] + a1r[s, 1, j].astype(F32)).astype(BF16)
            second.append(links.push(a2s.at[s], a2r.at[s], ring(far, b)))
        yield

        for s in range(2):
            first[s, 0].wait_recv()
            second[s].wait_recv()
            for j in range(2):
                accb[2 * s + j] = (
                    acc[a, 2 * s + j] + a1r[s, 0, j].astype(F32) + a2r[s, j].astype(F32)
                )

        steps = ((flip(b), 3 - b), (3 - b, flip(b)))
        bufs = (
            (b1s0, b1r0, b2s0, b2r0, slice(0, cut)),
            (b1s1, b1r1, b2s1, b2r1, slice(cut, width)),
        )
        first = {}
        for which in (1, 0):
            for s in range(2):
                near, far = steps[s]
                back = (3 - near, flip(near))[s]
                quarter = back if which else near
                s1, r1, s2, r2, cols = bufs[s]
                s1[which] = accb[quarter, :, cols].astype(BF16)
                first[s, which] = links.push(s1.at[which], r1.at[which], ring(a, near))
        yield

        second = []
        for s in range(2):
            near, far = steps[s]
            s1, r1, s2, r2, cols = bufs[s]
            first[s, 1].wait_recv()
            s2[...] = (accb[far, :, cols] + r1[1].astype(F32)).astype(BF16)
            second.append(links.push(s2, r2, ring(a, far)))
        yield

        per = zf.shape[1] // 8
        zf[...] = jnp.zeros(zf.shape, F32)
        for s in range(2):
            s1, r1, s2, r2, cols = bufs[s]
            first[s, 0].wait_recv()
            second[s].wait_recv()
            done = accb[b, :, cols] + r1[0].astype(F32) + r2[...].astype(F32)
            for k in range(cols.start // COLS, cols.stop // COLS):
                at_col = k * COLS - cols.start
                for g in range(groups):
                    n = k * groups + g
                    zf[n // per, (n % per) * 8 : (n % per) * 8 + 8, :] = done[
                        g * 8 : g * 8 + 8, at_col : at_col + COLS
                    ]

        zs[...] = zf[...].astype(BF16)
        turn, arrived = links.group(zr.at[pl.ds(0, nz - 1)], beside_z[0])
        for k in range(1, nz):
            turn(zs.at[(z + k) % nz], zr.at[z], at(x, y, (z + k) % nz, c))
        yield

        arrived()
        total = zf[z]
        for k in range(1, nz):
            total = total + zr[(z + nz - k) % nz].astype(F32)
        zg[z] = total.astype(BF16)
        turn, arrived = links.group(zg.at[pl.ds(0, nz - 1)], beside_z[0])
        for k in range(1, nz):
            turn(zg.at[z], zg.at[z], at(x, y, (z + k) % nz, c))
        yield

        arrived()
        zf[...] = zg[...].astype(F32)
        for k in range(width // COLS):
            pieces = []
            for g in range(groups):
                n = k * groups + g
                pieces.append(zf[n // per, (n % per) * 8 : (n % per) * 8 + 8, :])
            r[c, a, b, :, k * COLS : (k + 1) * COLS] = jnp.concatenate(pieces, axis=0).astype(BF16)

        across, all_across = links.group(r.at[1 - c], sibling)
        shared.append(all_across)

        def share(a_, b_):
            across(r.at[c, a_, b_], r.at[c, a_, b_], sibling)
            square(number, c, a_, b_)

        def along_a(b_):
            block = r.at[c, a, b_]
            return (
                links.push(block, block, ring(wrap(a + 1), b)),
                links.push(block, block, ring(wrap(a - 1), b)),
            )

        block = r.at[c, a, b]
        to_next = links.push(block, block, ring(a, wrap(b + 1)))
        to_last = links.push(block, block, ring(a, wrap(b - 1)))
        wide = [along_a(b)]
        share(a, b)
        yield

        to_next.wait_recv()
        block = r.at[c, a, wrap(b - 1), top]
        on_next = links.push(block, block, ring(a, wrap(b + 1)))
        wide.append(along_a(wrap(b - 1)))
        share(a, wrap(b - 1))
        to_last.wait_recv()
        block = r.at[c, a, wrap(b + 1), bottom]
        on_last = links.push(block, block, ring(a, wrap(b - 1)))
        wide.append(along_a(wrap(b + 1)))
        share(a, wrap(b + 1))
        yield

        on_next.wait_recv()
        on_last.wait_recv()
        wide.append(along_a(wrap(b + 2)))
        share(a, wrap(b + 2))
        yield

        order = (b, wrap(b - 1), wrap(b + 1), wrap(b + 2))
        rest = []
        for k, b_ in enumerate(order):
            wide[k][0].wait_recv()
            if k < 2:
                block = r.at[c, wrap(a - 1), b_]
                rest.append(links.push(block, block, ring(wrap(a + 1), b)))
            share(wrap(a - 1), b_)
            wide[k][1].wait_recv()
            if k >= 2:
                block = r.at[c, wrap(a + 1), b_]
                rest.append(links.push(block, block, ring(wrap(a - 1), b)))
            share(wrap(a + 1), b_)
            yield
        for k, b_ in enumerate(order):
            rest[k].wait_recv()
            share(wrap(a + 2), b_)
            yield

    going = [stream(k, *refs) for k, refs in enumerate(streams)]

    def step():
        for one in going:
            next(one, None)

    step()
    hear(2)

    tn = (((0,), (0,)), ((), ()))
    dpatch[...] = lax.dot_general(
        glow[0:CLS, :], w[...], tn, preferred_element_type=F32
    ) + lax.dot_general(glow[CLS:PAD_OUTS, :], wbs[...], tn, preferred_element_type=F32)

    def reach(row_tap, here):
        total = None
        for col_tap in range(3):
            k = (3 * row_tap + col_tap) * DEPTH
            piece = shifted(dpatch[here * COLS : (here + 1) * COLS, k : k + DEPTH], 2 - col_tap)
            total = piece if total is None else total + piece
        return total

    edge_s[0] = reach(0, 0)
    edge_s[1] = reach(2, 1)
    edge_out = links.make(edge_s.at[c], edge_r.at[1 - c], outer)
    edge_in = links.push(edge_s.at[1 - c], edge_r.at[c], sibling)

    @pl.when(has_outer)
    def _():
        edge_out.start()

    @pl.when(jnp.logical_not(has_outer))
    def _():
        edge_r[c] = jnp.zeros(edge_r.shape[1:], F32)

    sums = lax.dot_general(
        jnp.ones((8, 2 * COLS), F32), gf[...], nt,
        precision=lax.Precision.HIGHEST, preferred_element_type=F32,
    )
    lane = lax.broadcasted_iota(jnp.int32, (1, COLS), 1)
    mine = jnp.zeros((8, COLS), F32)
    rows8 = lax.broadcasted_iota(jnp.int32, (8, COLS), 0)
    for k in range(PAD_OUTS // COLS):
        mine = jnp.where(rows8 == k, sums[:, k * COLS : (k + 1) * COLS], mine)
    scalars = (jnp.sum(focal_sum), jnp.sum(giou), jnp.sum(positive))
    for k, value in enumerate(scalars):
        mine = jnp.where((rows8 == 6) & (lane == k), value, mine)
    stages = (sibling,) + tuple(ring(n, b) for n in (flip(a), 3 - a)) + tuple(
        ring(a, n) for n in (flip(b), 3 - b)
    )
    doubling = []

    def double(k):
        if k == 0:
            small[0, 0] = mine
        else:
            doubling[k - 1].wait_recv()
            small[k, 0] = small[k - 1, 0] + small[k - 1, 1]
        doubling.append(links.push(small.at[k, 0], small.at[k, 1], stages[k]))

    double(0)
    step()
    double(1)

    tg_own = (reach(1, 0) + reach(0, 1), reach(2, 0) + reach(1, 1))
    edge_in.wait_recv()

    @pl.when(has_outer)
    def _():
        edge_out.wait_recv()

    for here in range(2):
        tg_out[0, here] = (tg_own[here] + edge_r[here]).astype(BF16)

    step()
    double(2)
    step()
    double(3)
    step()
    double(4)
    step()
    doubling[4].wait_recv()
    sz[z] = small[4, 0] + small[4, 1]
    turn, small_arrived = links.group(sz.at[pl.ds(0, nz - 1)], beside_z[0])
    for k in range(1, nz):
        turn(sz.at[z], sz.at[z], at(x, y, (z + k) % nz, c))
    step()
    step()
    step()
    for _ in range(2 * RING + 1):
        step()

    small_arrived()
    whole = sz[0]
    for k in range(1, nz):
        whole = whole + sz[k]
    s_out[...] = whole

    for all_across in shared:
        all_across()

    def other(i, carry):
        for k in range(len(STREAMS)):
            square(k, 1 - c, i // RING, i % RING)
        return carry

    lax.fori_loop(0, RING * RING, other, 0)
    links.drain()

    @pl.when(has_outer)
    def _():
        halo.wait_send()
        edge_out.wait_send()


def scale_kernel(r0, r1, q, s, tg, cls_out, box_out, loss_out, cls_bias_out, box_bias_out, tg_out, stage, sem):
    slots = stage.shape[0]
    tower_copy = pltpu.make_async_copy(tg, tg_out, sem.at[slots])
    tower_copy.start()
    rows8 = lax.broadcasted_iota(jnp.int32, (8, COLS), 0)
    bias = jnp.where(rows8 < PAD_OUTS // COLS, s[...], 0.0)
    total = bias * bias
    for k in range(len(STREAMS)):
        for n in range(2 * RING * RING):
            total = total + q[k, n // (RING * RING), n // RING % RING, n % RING]
    total = jnp.sum(total, keepdims=True)
    scale = lax.rsqrt(total / (OUTS * (WIDTH + 1)) + NORM_EPS)
    bias = bias * scale
    cls_bias_out[...] = bias
    at_row, at_lane = CLS // COLS, CLS % COLS
    box_bias_out[...] = pltpu.roll(bias, COLS - at_lane, 1)[at_row : at_row + 1, 0 : OUTS - CLS]
    loss_out[...] = (s[6:7, 0:1] + s[6:7, 1:2]) / s[6:7, 2:3]

    count = CLS // BLOCK

    def store(k):
        return pltpu.make_async_copy(
            stage.at[k % slots],
            cls_out.at[pl.ds(pl.multiple_of(k * BLOCK, BLOCK), BLOCK)],
            sem.at[k % slots],
        )

    def chunk(k, carry):
        @pl.when(k >= slots)
        def _():
            store(k - slots).wait()

        for h in range(2):
            for r, (start, stop, _) in zip((r0, r1), STREAMS):
                stage[k % slots, :, h * HALF + start : h * HALF + stop] = (
                    r[h, k // RING, k % RING].astype(F32) * scale
                )
        store(k).start()
        return carry

    lax.fori_loop(0, count, chunk, 0)
    for h in range(2):
        for r, (start, stop, _) in zip((r0, r1), STREAMS):
            box_out[:, h * HALF + start : h * HALF + stop] = (
                r[h, RING - 1, RING - 1].astype(F32) * scale
            )[0 : 4 * ANCHORS]
    for k in range(count - slots, count):
        store(k).wait()
    tower_copy.wait()


def per_device(
    zl_count, zh_count, tower, cls_weight, cls_bias, box_weight, box_bias, labels, target_index, boxes
):
    nz = zl_count * zh_count
    vmem = pl.BlockSpec(memory_space=pltpu.VMEM)

    def buf(*shape, dtype=BF16):
        return pltpu.VMEM(shape, dtype)

    per_stream = []
    for start, stop, cut in STREAMS:
        width = stop - start
        per = -(-(BLOCK // 8 * (width // COLS)) // nz) * 8
        per_stream += [
            buf(RING, RING, BLOCK, width, dtype=F32),
            buf(2, 2, 2, BLOCK, width),
            buf(2, 2, 2, BLOCK, width),
            buf(2, 2, BLOCK, width),
            buf(2, 2, BLOCK, width),
            buf(RING, BLOCK, width, dtype=F32),
        ]
        for part in (cut, width - cut):
            per_stream += [buf(2, BLOCK, part)] * 2 + [buf(BLOCK, part)] * 2
        per_stream += [buf(nz, per, COLS, dtype=F32)] + [buf(nz, per, COLS)] * 3

    r0, r1, q, s, tower_grad = pl.pallas_call(
        functools.partial(step_kernel, zl_count, zh_count),
        out_shape=(
            buf(2, RING, RING, BLOCK, STREAMS[0][1] - STREAMS[0][0]),
            buf(2, RING, RING, BLOCK, STREAMS[1][1] - STREAMS[1][0]),
            buf(len(STREAMS), 2, RING, RING, 8, COLS, dtype=F32),
            buf(8, COLS, dtype=F32),
            buf(*tower.shape),
        ),
        in_specs=[
            vmem,
            pl.BlockSpec(memory_space=pl.ANY),
            vmem, vmem, vmem, vmem, vmem,
            pl.BlockSpec(memory_space=pltpu.SMEM),
        ],
        out_specs=(vmem, vmem, vmem, vmem, vmem),
        scratch_shapes=[
            buf(CLS, WIDTH),
            buf(PAD_OUTS - CLS, WIDTH),
            buf(8, PAD_OUTS, dtype=F32),
            buf(6, COLS, DEPTH),
            buf(2, 2 * COLS, HALF),
            buf(2 * COLS, HALF),
            buf(PAD_OUTS, 2 * COLS, dtype=F32),
            buf(PAD_OUTS, 2 * COLS, dtype=F32),
            buf(PAD_OUTS, 2 * COLS),
            buf(PAD_OUTS, 2 * COLS),
            buf(2, PAD_OUTS - CLS, COLS, dtype=F32),
            buf(5, 2, 8, COLS, dtype=F32),
            buf(nz, 8, COLS, dtype=F32),
            buf(2 * COLS, WIDTH, dtype=F32),
            buf(2, COLS, DEPTH, dtype=F32),
            buf(2, COLS, DEPTH, dtype=F32),
            pltpu.SemaphoreType.DMA,
            pltpu.SemaphoreType.REGULAR((max(nz // 2 - 1, 1),)),
            pltpu.SemaphoreType.DMA((IN_FLIGHT + GROUPS,)),
            pltpu.SemaphoreType.DMA((RECEIVES,)),
            *per_stream,
        ],
        compiler_params=pltpu.CompilerParams(
            collective_id=0, has_side_effects=True, vmem_limit_bytes=56 * 2**20
        ),
        name="step",
    )(tower, cls_weight, box_weight, cls_bias, box_bias, labels, target_index, boxes)

    hbm = pl.BlockSpec(memory_space=pl.ANY)
    cls_grad, box_grad, loss, cls_bias_grad, box_bias_grad, tower_grad = pl.pallas_call(
        scale_kernel,
        out_shape=(
            jax.ShapeDtypeStruct((CLS, WIDTH), F32),
            jax.ShapeDtypeStruct((OUTS - CLS, WIDTH), F32),
            jax.ShapeDtypeStruct((1, 1), F32),
            jax.ShapeDtypeStruct((8, COLS), F32),
            jax.ShapeDtypeStruct((1, OUTS - CLS), F32),
            jax.ShapeDtypeStruct(tower.shape, BF16),
        ),
        in_specs=[vmem, vmem, vmem, vmem, vmem],
        out_specs=(hbm, vmem, vmem, vmem, vmem, hbm),
        scratch_shapes=[
            buf(4, BLOCK, WIDTH, dtype=F32),
            pltpu.SemaphoreType.DMA((5,)),
        ],
        compiler_params=pltpu.CompilerParams(vmem_limit_bytes=40 * 2**20),
        name="scale",
    )(r0, r1, q, s, tower_grad)
    return (
        loss.reshape(()),
        cls_grad,
        cls_bias_grad.reshape(-1)[:CLS],
        box_grad,
        box_bias_grad.reshape(-1),
        tower_grad,
    )


def solution(mesh):
    zl_count = mesh.shape["tile"] // (2 * RING)
    zh_count = mesh.shape["img"] // RING
    placed = (
        P("img", "tile", None, None),
        P(),
        P(),
        P(),
        P(),
        P("img", None, "tile", None),
        P("img", None, "tile", None),
        P("img", None, None),
    )
    return jax.shard_map(
        functools.partial(per_device, zl_count, zh_count),
        mesh=mesh,
        in_specs=placed,
        out_specs=(P(), P(), P(), P(), P(), P("img", "tile", None, None)),
        check_vma=False,
    )
```

time: 75.4 us -> 66.7 us (0.88)
  Pallas kernels: 74.1 us -> 65.9 us
    pallas_call x1, Pallas kernels: 69.6 us -> 61.4 us  [per_device(): pl.pallas_call(functools.partial(step_kernel, zl_count, zh_count), out_sh...]
where the time goes in v3:
time: 66.7 us; the launch traced here: 66.5 us
  Pallas kernels  65.9 us (99%)
    pallas_call x1, Pallas kernels, per_device(): pl.pallas_call(functools.partial(step_kernel, zl_count, zh_count), out_sh...  61.4 us
    pallas_call x1, Pallas kernels, per_device(): pl.pallas_call(scale_kernel, out_shape=(jax.ShapeDtypeStruct((CLS, WIDTH)...  4.51 us

profile of v3, /device:TPU:1, one launch (start us, length us, event | category | flops | bytes accessed | tf_op | source)
XLA Modules:
  0.0 66.5 jit_solution(10304643628643513496)
XLA Ops:
  0.6 61.4 %step.1 = (bf16[2,4,4,48,640]{4,3,2,1,0:T(8,128)(2,1)S(1)}, bf16[2,4,4,48,512]{4,3,2,1,0:T(8,128)(2,1)S(1)}, f32[2,2,4,4,8,128]{5,4,3,2,1,0:T(8,128)S(1)}, f32[8...) custom-call(bf16[1,2,128,256]{3,2,1,0:T(8,128)(2,1)} %tower.1, bf16[720,2304]{1,0:T(8,128)(2,1)} %wc_hbm.1, ...), custom_call_target="tpu_custom_call" | custom-call | tf_op jit(solution)/shard_map/step/pallas_call | solution.py:743
  62.0 4.5 %scale.1 = (f32[720,2304]{1,0:T(8,128)}, f32[36,2304]{1,0:T(8,128)}, f32[1,1]{1,0:T(1,128)}, f32[8,128]{1,0:T(8,128)}, f32[1,36]{1,0:T(1,128)}, /*index=5*/bf16[1,2,128,256]{3,2,1,0:T(8,128)(2,1)}) custom-call(bf16[2,4,4,48,640]{4,3,2,1,0:T(8,128)(2,1)S(1)} %get-tuple-element.17.r0, bf16[2,4,4,48,512]{4,3,2,1,0:T(8,128)(2,1)S(1)} %get-tuple-element.18.r1, ...), custom_call_target="tpu_custom_call" | custom-call | tf_op jit(solution)/shard_map/scale/pallas_call | solution.py:789

commit v4 on v3

--- a/solution.py
+++ b/solution.py
@@ -16,8 +16,8 @@
 
 RING = 4
 IN_FLIGHT = 40
-RECEIVES = 74
-GROUPS = 9
+RECEIVES = 62
+GROUPS = 11
 CLS = ANCHORS * CLASSES
 OUTS = CLS + 4 * ANCHORS
 PAD_OUTS = 768
@@ -27,7 +27,7 @@
 HALF = WIDTH // 2
 COLS = 128
 BLOCK = PAD_OUTS // (RING * RING)
-STREAMS = ((0, 640, 384), (640, 1152, 256))
+STREAMS = ((0, 640), (640, 1152))
 BF16 = jnp.bfloat16
 F32 = jnp.float32
 MESH = pl.DeviceIdType.MESH
@@ -151,11 +151,12 @@
 
 def step_kernel(
     zl_count, zh_count,
-    tower, wc_hbm, wb, cls_bias, box_bias, labels, tindex, boxes,
+    tower_in, wc_in, wb_in, cls_bias_in, box_bias_in, labels_in, tindex_in, boxes_in,
     r_out0, r_out1, q_out, s_out, tg_out,
-    w, wbs, bias_row, ext, patches, beside, outs, gf, glow, theirs, boxy,
+    tower, w, wb, cls_bias, box_bias, labels, tindex, boxes,
+    wbs, bias_row, ext, patches, beside, outs, gf, glow, theirs, boxy,
     small, sz, dpatch, edge_s, edge_r,
-    wsem, ready, send, recv, *per_stream,
+    load_sem, ready, across_b, send, recv, *per_stream,
 ):
     t = lax.axis_index("tile")
     m = lax.axis_index("img")
@@ -183,9 +184,6 @@
     has_outer = jnp.where(c == 0, t > 0, t < tiles - 1)
     links = Links(send, recv)
 
-    load = pltpu.make_async_copy(wc_hbm, w, wsem)
-    load.start()
-
     barrier = pltpu.get_barrier_semaphore()
 
     def greet(device):
@@ -203,6 +201,18 @@
     @pl.when(has_outer)
     def _():
         greet(outer)
+
+    loads = [
+        pltpu.make_async_copy(src, dst, load_sem.at[k])
+        for k, (src, dst) in enumerate((
+            (tindex_in, tindex), (boxes_in, boxes), (tower_in, tower), (wb_in, wb),
+            (wc_in, w), (cls_bias_in, cls_bias), (box_bias_in, box_bias), (labels_in, labels),
+        ))
+    ]
+    for load in loads:
+        load.start()
+    for load in loads[:4]:
+        load.wait()
 
     wanted = jnp.concatenate([tindex[0, :, 0, :], tindex[0, :, 1, :]], axis=1)
 
@@ -268,6 +278,8 @@
 
     rows_across = links.push(tower.at[0], ext.at[pl.ds(1 + 2 * c, 2)], sibling)
     tell(0)
+    for near in (flip(b), 3 - b):
+        pl.semaphore_signal(across_b, inc=1, device_id=ring(a, near), device_id_type=MESH)
 
     nt = (((1,), (1,)), ((), ()))
 
@@ -281,11 +293,12 @@
     edge = 3 * DEPTH
     patches[0, 0:COLS, 0:edge] = jnp.zeros((COLS, edge), BF16)
     patches[1, COLS : 2 * COLS, HALF - edge : HALF] = jnp.zeros((COLS, edge), BF16)
+    for load in loads[4:]:
+        load.wait()
     bias_row[0:1, 0:CLS] = cls_bias[...].reshape(1, CLS)
     bias_row[0:1, CLS:OUTS] = box_bias[...].reshape(1, OUTS - CLS)
     bias_row[0:1, OUTS:PAD_OUTS] = jnp.zeros((1, PAD_OUTS - OUTS), F32)
     bias_col = column(bias_row[0:1, :])
-    load.wait()
     for lhs, rows in ((w, slice(0, CLS)), (wbs, slice(CLS, PAD_OUTS))):
         outs[rows, :] = (
             product(lhs[:, 0:HALF], patches[0])
@@ -356,9 +369,9 @@
 
     streams = []
     each = len(per_stream) // len(STREAMS)
-    for k, (start, stop, cut) in enumerate(STREAMS):
-        streams.append(((r_out0, r_out1)[k], start, stop, cut, *per_stream[k * each : (k + 1) * each]))
-    for _, start, stop, _, acc, *_ in streams:
+    for k, (start, stop) in enumerate(STREAMS):
+        streams.append(((r_out0, r_out1)[k], start, stop, *per_stream[k * each : (k + 1) * each]))
+    for _, start, stop, acc, *_ in streams:
         part = jnp.dot(glow[...], patches[c, :, start:stop], preferred_element_type=F32)
         acc[...] = part.reshape(acc.shape)
     hear(1)
@@ -375,7 +388,7 @@
     def wrap(i):
         return (i + RING) % RING
 
-    top, bottom = slice(0, 32), slice(32, BLOCK)
+    far_first = sorted(range(1, nz), key=lambda k: -min(k, nz - k))
     groups = BLOCK // 8
     shared = []
 
@@ -389,9 +402,8 @@
         q_out[k, h, a_, b_] = total
 
     def stream(
-        number, r, start, stop, cut,
-        acc, a1s, a1r, a2s, a2r, accb, b1s0, b1r0, b2s0, b2r0, b1s1, b1r1, b2s1, b2r1,
-        zf, zs, zr, zg,
+        number, r, start, stop,
+        acc, a1s, a1r, a2s, a2r, accb, b_s, b_r, zf, zs, zr, zg,
     ):
         width = stop - start
         part = jnp.dot(theirs[...], beside[:, start:stop], preferred_element_type=F32)
@@ -426,49 +438,26 @@
                     acc[a, 2 * s + j] + a1r[s, 0, j].astype(F32) + a2r[s, j].astype(F32)
                 )
 
-        steps = ((flip(b), 3 - b), (3 - b, flip(b)))
-        bufs = (
-            (b1s0, b1r0, b2s0, b2r0, slice(0, cut)),
-            (b1s1, b1r1, b2s1, b2r1, slice(cut, width)),
-        )
-        first = {}
-        for which in (1, 0):
-            for s in range(2):
-                near, far = steps[s]
-                back = (3 - near, flip(near))[s]
-                quarter = back if which else near
-                s1, r1, s2, r2, cols = bufs[s]
-                s1[which] = accb[quarter, :, cols].astype(BF16)
-                first[s, which] = links.push(s1.at[which], r1.at[which], ring(a, near))
-        yield
-
-        second = []
-        for s in range(2):
-            near, far = steps[s]
-            s1, r1, s2, r2, cols = bufs[s]
-            first[s, 1].wait_recv()
-            s2[...] = (accb[far, :, cols] + r1[1].astype(F32)).astype(BF16)
-            second.append(links.push(s2, r2, ring(a, far)))
+        turn, arrived = links.group(b_r, ring(a, wrap(b + 1)))
+        for k in (2, 1, 3):
+            b_s[k - 1] = accb[wrap(b + k)].astype(BF16)
+            turn(b_s.at[k - 1], b_r.at[k - 1], ring(a, wrap(b + k)))
         yield
 
         per = zf.shape[1] // 8
         zf[...] = jnp.zeros(zf.shape, F32)
-        for s in range(2):
-            s1, r1, s2, r2, cols = bufs[s]
-            first[s, 0].wait_recv()
-            second[s].wait_recv()
-            done = accb[b, :, cols] + r1[0].astype(F32) + r2[...].astype(F32)
-            for k in range(cols.start // COLS, cols.stop // COLS):
-                at_col = k * COLS - cols.start
-                for g in range(groups):
-                    n = k * groups + g
-                    zf[n // per, (n % per) * 8 : (n % per) * 8 + 8, :] = done[
-                        g * 8 : g * 8 + 8, at_col : at_col + COLS
-                    ]
+        arrived()
+        done = accb[b] + b_r[0].astype(F32) + b_r[1].astype(F32) + b_r[2].astype(F32)
+        for k in range(width // COLS):
+            for g in range(groups):
+                n = k * groups + g
+                zf[n // per, (n % per) * 8 : (n % per) * 8 + 8, :] = done[
+                    g * 8 : g * 8 + 8, k * COLS : (k + 1) * COLS
+                ]
 
         zs[...] = zf[...].astype(BF16)
         turn, arrived = links.group(zr.at[pl.ds(0, nz - 1)], beside_z[0])
-        for k in range(1, nz):
+        for k in far_first:
             turn(zs.at[(z + k) % nz], zr.at[z], at(x, y, (z + k) % nz, c))
         yield
 
@@ -478,7 +467,7 @@
             total = total + zr[(z + nz - k) % nz].astype(F32)
         zg[z] = total.astype(BF16)
         turn, arrived = links.group(zg.at[pl.ds(0, nz - 1)], beside_z[0])
-        for k in range(1, nz):
+        for k in far_first:
             turn(zg.at[z], zg.at[z], at(x, y, (z + k) % nz, c))
         yield
 
@@ -506,26 +495,18 @@
             )
 
         block = r.at[c, a, b]
-        to_next = links.push(block, block, ring(a, wrap(b + 1)))
-        to_last = links.push(block, block, ring(a, wrap(b - 1)))
         wide = [along_a(b)]
+        to = {k: links.push(block, block, ring(a, wrap(b + k))) for k in (1, 3, 2)}
         share(a, b)
         yield
 
-        to_next.wait_recv()
-        block = r.at[c, a, wrap(b - 1), top]
-        on_next = links.push(block, block, ring(a, wrap(b + 1)))
-        wide.append(along_a(wrap(b - 1)))
-        share(a, wrap(b - 1))
-        to_last.wait_recv()
-        block = r.at[c, a, wrap(b + 1), bottom]
-        on_last = links.push(block, block, ring(a, wrap(b - 1)))
-        wide.append(along_a(wrap(b + 1)))
-        share(a, wrap(b + 1))
+        for k in (1, 3):
+            to[k].wait_recv()
+            wide.append(along_a(wrap(b - k)))
+            share(a, wrap(b - k))
         yield
 
-        on_next.wait_recv()
-        on_last.wait_recv()
+        to[2].wait_recv()
         wide.append(along_a(wrap(b + 2)))
         share(a, wrap(b + 2))
         yield
@@ -623,6 +604,7 @@
     for here in range(2):
         tg_out[0, here] = (tg_own[here] + edge_r[here]).astype(BF16)
 
+    pl.semaphore_wait(across_b, 2)
     step()
     double(2)
     step()
@@ -633,9 +615,8 @@
     doubling[4].wait_recv()
     sz[z] = small[4, 0] + small[4, 1]
     turn, small_arrived = links.group(sz.at[pl.ds(0, nz - 1)], beside_z[0])
-    for k in range(1, nz):
+    for k in far_first:
         turn(sz.at[z], sz.at[z], at(x, y, (z + k) % nz, c))
-    step()
     step()
     step()
     for _ in range(2 * RING + 1):
@@ -697,7 +678,7 @@
             store(k - slots).wait()
 
         for h in range(2):
-            for r, (start, stop, _) in zip((r0, r1), STREAMS):
+            for r, (start, stop) in zip((r0, r1), STREAMS):
                 stage[k % slots, :, h * HALF + start : h * HALF + stop] = (
                     r[h, k // RING, k % RING].astype(F32) * scale
                 )
@@ -706,7 +687,7 @@
 
     lax.fori_loop(0, count, chunk, 0)
     for h in range(2):
-        for r, (start, stop, _) in zip((r0, r1), STREAMS):
+        for r, (start, stop) in zip((r0, r1), STREAMS):
             box_out[:, h * HALF + start : h * HALF + stop] = (
                 r[h, RING - 1, RING - 1].astype(F32) * scale
             )[0 : 4 * ANCHORS]
@@ -720,12 +701,13 @@
 ):
     nz = zl_count * zh_count
     vmem = pl.BlockSpec(memory_space=pltpu.VMEM)
+    hbm = pl.BlockSpec(memory_space=pl.ANY)
 
     def buf(*shape, dtype=BF16):
         return pltpu.VMEM(shape, dtype)
 
     per_stream = []
-    for start, stop, cut in STREAMS:
+    for start, stop in STREAMS:
         width = stop - start
         per = -(-(BLOCK // 8 * (width // COLS)) // nz) * 8
         per_stream += [
@@ -736,8 +718,7 @@
             buf(2, 2, BLOCK, width),
             buf(RING, BLOCK, width, dtype=F32),
         ]
-        for part in (cut, width - cut):
-            per_stream += [buf(2, BLOCK, part)] * 2 + [buf(BLOCK, part)] * 2
+        per_stream += [buf(RING - 1, BLOCK, width)] * 2
         per_stream += [buf(nz, per, COLS, dtype=F32)] + [buf(nz, per, COLS)] * 3
 
     r0, r1, q, s, tower_grad = pl.pallas_call(
@@ -749,15 +730,17 @@
             buf(8, COLS, dtype=F32),
             buf(*tower.shape),
         ),
-        in_specs=[
-            vmem,
-            pl.BlockSpec(memory_space=pl.ANY),
-            vmem, vmem, vmem, vmem, vmem,
-            pl.BlockSpec(memory_space=pltpu.SMEM),
-        ],
+        in_specs=[hbm] * 8,
         out_specs=(vmem, vmem, vmem, vmem, vmem),
         scratch_shapes=[
+            buf(*tower.shape),
             buf(CLS, WIDTH),
+            buf(*box_weight.shape),
+            buf(*cls_bias.shape, dtype=F32),
+            buf(*box_bias.shape, dtype=F32),
+            buf(*labels.shape, dtype=jnp.int32),
+            buf(*target_index.shape, dtype=jnp.int32),
+            pltpu.SMEM(boxes.shape, F32),
             buf(PAD_OUTS - CLS, WIDTH),
             buf(8, PAD_OUTS, dtype=F32),
             buf(6, COLS, DEPTH),
@@ -773,8 +756,9 @@
             buf(2 * COLS, WIDTH, dtype=F32),
             buf(2, COLS, DEPTH, dtype=F32),
             buf(2, COLS, DEPTH, dtype=F32),
-            pltpu.SemaphoreType.DMA,
+            pltpu.SemaphoreType.DMA((8,)),
             pltpu.SemaphoreType.REGULAR((max(nz // 2 - 1, 1),)),
+            pltpu.SemaphoreType.REGULAR,
             pltpu.SemaphoreType.DMA((IN_FLIGHT + GROUPS,)),
             pltpu.SemaphoreType.DMA((RECEIVES,)),
             *per_stream,
@@ -785,7 +769,6 @@
         name="step",
     )(tower, cls_weight, box_weight, cls_bias, box_bias, labels, target_index, boxes)
 
-    hbm = pl.BlockSpec(memory_space=pl.ANY)
     cls_grad, box_grad, loss, cls_bias_grad, box_bias_grad, tower_grad = pl.pallas_call(
         scale_kernel,
         out_shape=(

time: 66.7 us -> 62.9 us (0.943)
  Pallas kernels: 65.9 us -> 62.1 us
    pallas_call x1, Pallas kernels: 61.4 us -> 57.6 us  [per_device(): pl.pallas_call(functools.partial(step_kernel, zl_count, zh_count), out_sh...]
where the time goes in v4:
time: 62.9 us; the launch traced here: 62.7 us
  Pallas kernels  62.1 us (99%)
  between operations  0.64 us (1%)
    pallas_call x1, Pallas kernels, per_device(): pl.pallas_call(functools.partial(step_kernel, zl_count, zh_count), out_sh...  57.6 us
    pallas_call x1, Pallas kernels, per_device(): pl.pallas_call(scale_kernel, out_shape=(jax.ShapeDtypeStruct((CLS, WIDTH)...  4.51 us

profile of v4, /device:TPU:1, one launch (start us, length us, event | category | flops | bytes accessed | tf_op | source)
XLA Modules:
  0.0 62.7 jit_solution(6495880895335903525)
XLA Ops:
  0.6 57.6 %step.1 = (bf16[2,4,4,48,640]{4,3,2,1,0:T(8,128)(2,1)S(1)}, bf16[2,4,4,48,512]{4,3,2,1,0:T(8,128)(2,1)S(1)}, f32[2,2,4,4,8,128]{5,4,3,2,1,0:T(8,128)S(1)}, f32[8...) custom-call(bf16[1,2,128,256]{3,2,1,0:T(8,128)(2,1)} %tower_in.1, bf16[720,2304]{1,0:T(8,128)(2,1)} %wc_in.1, ...), custom_call_target="tpu_custom_call" | custom-call | tf_op jit(solution)/shard_map/step/pallas_call | solution.py:724
  58.2 4.5 %scale.1 = (f32[720,2304]{1,0:T(8,128)}, f32[36,2304]{1,0:T(8,128)}, f32[1,1]{1,0:T(1,128)}, f32[8,128]{1,0:T(8,128)}, f32[1,36]{1,0:T(1,128)}, /*index=5*/bf16[1,2,128,256]{3,2,1,0:T(8,128)(2,1)}) custom-call(bf16[2,4,4,48,640]{4,3,2,1,0:T(8,128)(2,1)S(1)} %get-tuple-element.17.r0, bf16[2,4,4,48,512]{4,3,2,1,0:T(8,128)(2,1)S(1)} %get-tuple-element.18.r1, ...), custom_call_target="tpu_custom_call" | custom-call | tf_op jit(solution)/shard_map/scale/pallas_call | solution.py:772

commit v5 on v4

--- a/solution.py
+++ b/solution.py
@@ -15,9 +15,9 @@
 NORM_EPS = 1e-06
 
 RING = 4
-IN_FLIGHT = 40
-RECEIVES = 62
-GROUPS = 11
+IN_FLIGHT = 32
+RECEIVES = 85
+GROUPS = 18
 CLS = ANCHORS * CLASSES
 OUTS = CLS + 4 * ANCHORS
 PAD_OUTS = 768
@@ -27,7 +27,7 @@
 HALF = WIDTH // 2
 COLS = 128
 BLOCK = PAD_OUTS // (RING * RING)
-STREAMS = ((0, 640), (640, 1152))
+STREAMS = ((0, 384), (384, 768), (768, 1152))
 BF16 = jnp.bfloat16
 F32 = jnp.float32
 MESH = pl.DeviceIdType.MESH
@@ -152,12 +152,15 @@
 def step_kernel(
     zl_count, zh_count,
     tower_in, wc_in, wb_in, cls_bias_in, box_bias_in, labels_in, tindex_in, boxes_in,
-    r_out0, r_out1, q_out, s_out, tg_out,
-    tower, w, wb, cls_bias, box_bias, labels, tindex, boxes,
-    wbs, bias_row, ext, patches, beside, outs, gf, glow, theirs, boxy,
-    small, sz, dpatch, edge_s, edge_r,
-    load_sem, ready, across_b, send, recv, *per_stream,
+    *refs,
 ):
+    r_outs, (s_out, tg_out), refs = refs[: len(STREAMS)], refs[len(STREAMS) :][:2], refs[len(STREAMS) + 2 :]
+    (
+        tower, w, wb, cls_bias, box_bias, labels, tindex, boxes,
+        wbs, bias_row, ext, patches, beside, outs, gf, glow, theirs, boxy,
+        small_c, small_a, small_b, sz, dpatch, edge_s, edge_r,
+        load_sem, ready, across_a, across_b, send, recv, *per_stream,
+    ) = refs
     t = lax.axis_index("tile")
     m = lax.axis_index("img")
     tiles = zl_count * RING * 2
@@ -278,6 +281,8 @@
 
     rows_across = links.push(tower.at[0], ext.at[pl.ds(1 + 2 * c, 2)], sibling)
     tell(0)
+    for near in (flip(a), 3 - a):
+        pl.semaphore_signal(across_a, inc=1, device_id=ring(near, b), device_id_type=MESH)
     for near in (flip(b), 3 - b):
         pl.semaphore_signal(across_b, inc=1, device_id=ring(a, near), device_id_type=MESH)
 
@@ -291,35 +296,47 @@
         return jnp.transpose(wide)[:, 0:1]
 
     edge = 3 * DEPTH
-    patches[0, 0:COLS, 0:edge] = jnp.zeros((COLS, edge), BF16)
-    patches[1, COLS : 2 * COLS, HALF - edge : HALF] = jnp.zeros((COLS, edge), BF16)
+    outer_part = (
+        (0, slice(0, COLS), slice(0, edge), slice(0, edge)),
+        (1, slice(COLS, 2 * COLS), slice(HALF - edge, HALF), slice(WIDTH - edge, WIDTH)),
+    )
     for load in loads[4:]:
         load.wait()
     bias_row[0:1, 0:CLS] = cls_bias[...].reshape(1, CLS)
     bias_row[0:1, CLS:OUTS] = box_bias[...].reshape(1, OUTS - CLS)
     bias_row[0:1, OUTS:PAD_OUTS] = jnp.zeros((1, PAD_OUTS - OUTS), F32)
     bias_col = column(bias_row[0:1, :])
-    for lhs, rows in ((w, slice(0, CLS)), (wbs, slice(CLS, PAD_OUTS))):
+    rows_across.wait_recv()
+    for half in range(2):
+
+        @pl.when(c == half)
+        def _():
+            part, positions, cols, _ = outer_part[half]
+            patches[part, positions, cols] = jnp.zeros((COLS, edge), BF16)
+            fill(ext[2 * half + 3 - 3 * half], 3 - 3 * half, (0, 1), put_own)
+
+    both = ((w, slice(0, CLS)), (wbs, slice(CLS, PAD_OUTS)))
+    for lhs, rows in both:
         outs[rows, :] = (
             product(lhs[:, 0:HALF], patches[0])
             + product(lhs[:, HALF:WIDTH], patches[1])
             + bias_col[rows]
         )
 
-    rows_across.wait_recv()
-
     @pl.when(has_outer)
     def _():
         halo.wait_recv()
 
     outer_across = links.push(ext.at[5 * c], ext.at[5 * c], sibling)
-    fill(ext[2 * c], 0, (0, 1), put_own)
-    fill(ext[2 * c + 3], 3, (0, 1), put_own)
-    for lhs, rows in ((w, slice(0, CLS)), (wbs, slice(CLS, PAD_OUTS))):
-        outs[rows, 0:COLS] += product(lhs[:, 0:edge], patches[0, 0:COLS, 0:edge])
-        outs[rows, COLS : 2 * COLS] += product(
-            lhs[:, WIDTH - edge : WIDTH], patches[1, COLS : 2 * COLS, HALF - edge : HALF]
-        )
+    for half in range(2):
+
+        @pl.when(c == half)
+        def _():
+            part, positions, cols, weights = outer_part[half]
+            fill(ext[5 * half], 3 * half, (0, 1), put_own)
+            for lhs, rows in both:
+                outs[rows, positions] += product(lhs[:, weights], patches[part, positions, cols])
+
     hear(0)
 
     class_ids = lax.broadcasted_iota(jnp.int32, (CLASSES, COLS), 0)
@@ -370,10 +387,14 @@
     streams = []
     each = len(per_stream) // len(STREAMS)
     for k, (start, stop) in enumerate(STREAMS):
-        streams.append(((r_out0, r_out1)[k], start, stop, *per_stream[k * each : (k + 1) * each]))
-    for _, start, stop, acc, *_ in streams:
+        streams.append((r_outs[k], start, stop, *per_stream[k * each : (k + 1) * each]))
+
+    def own_part(k):
+        _, start, stop, acc, *_ = streams[k]
         part = jnp.dot(glow[...], patches[c, :, start:stop], preferred_element_type=F32)
         acc[...] = part.reshape(acc.shape)
+
+    own_part(0)
     hear(1)
     outer_across.wait_recv()
     for half in range(2):
@@ -392,20 +413,15 @@
     groups = BLOCK // 8
     shared = []
 
-    def square(k, h, a_, b_):
-        r = streams[k][0]
-        value = r[h, a_, b_].astype(F32)
-        value = jnp.sum((value * value).reshape(groups, 8, value.shape[1]), axis=0)
-        total = value[:, 0:COLS]
-        for j in range(1, value.shape[1] // COLS):
-            total = total + value[:, j * COLS : (j + 1) * COLS]
-        q_out[k, h, a_, b_] = total
+    squares = []
 
     def stream(
         number, r, start, stop,
         acc, a1s, a1r, a2s, a2r, accb, b_s, b_r, zf, zs, zr, zg,
     ):
         width = stop - start
+        if number:
+            own_part(number)
         part = jnp.dot(theirs[...], beside[:, start:stop], preferred_element_type=F32)
         acc[...] += part.reshape(acc.shape)
 
@@ -466,6 +482,7 @@
         for k in range(1, nz):
             total = total + zr[(z + nz - k) % nz].astype(F32)
         zg[z] = total.astype(BF16)
+        squares.append(jnp.sum(total * total))
         turn, arrived = links.group(zg.at[pl.ds(0, nz - 1)], beside_z[0])
         for k in far_first:
             turn(zg.at[z], zg.at[z], at(x, y, (z + k) % nz, c))
@@ -485,7 +502,6 @@
 
         def share(a_, b_):
             across(r.at[c, a_, b_], r.at[c, a_, b_], sibling)
-            square(number, c, a_, b_)
 
         def along_a(b_):
             block = r.at[c, a, b_]
@@ -574,25 +590,36 @@
     rows8 = lax.broadcasted_iota(jnp.int32, (8, COLS), 0)
     for k in range(PAD_OUTS // COLS):
         mine = jnp.where(rows8 == k, sums[:, k * COLS : (k + 1) * COLS], mine)
-    scalars = (jnp.sum(focal_sum), jnp.sum(giou), jnp.sum(positive))
-    for k, value in enumerate(scalars):
-        mine = jnp.where((rows8 == 6) & (lane == k), value, mine)
-    stages = (sibling,) + tuple(ring(n, b) for n in (flip(a), 3 - a)) + tuple(
-        ring(a, n) for n in (flip(b), 3 - b)
-    )
-    doubling = []
-
-    def double(k):
-        if k == 0:
-            small[0, 0] = mine
+    def add_up(stage):
+        slots, here, devices = (
+            (small_c, c, (sibling,)),
+            (small_a, a, tuple(ring(wrap(a + k), b) for k in (2, 1, 3))),
+            (small_b, b, tuple(ring(a, wrap(b + k)) for k in (2, 1, 3))),
+            (sz, z, tuple(at(x, y, (z + k) % nz, c) for k in far_first)),
+        )[stage]
+        if stage == 0:
+            total = mine
+            scalars = (jnp.sum(focal_sum), jnp.sum(giou), jnp.sum(positive), sum(squares))
+            for n, value in enumerate(scalars):
+                total = jnp.where((rows8 == 6) & (lane == n), value, total)
         else:
-            doubling[k - 1].wait_recv()
-            small[k, 0] = small[k - 1, 0] + small[k - 1, 1]
-        doubling.append(links.push(small.at[k, 0], small.at[k, 1], stages[k]))
-
-    double(0)
+            total = added()
+        slots[here] = total
+        count = len(devices)
+        turn, arrived = links.group(slots.at[pl.ds(0, count)], devices[0])
+        for device in devices:
+            turn(slots.at[here], slots.at[here], device)
+
+        def result():
+            arrived()
+            total = slots[0]
+            for k in range(1, count + 1):
+                total = total + slots[k]
+            return total
+
+        return result
+
     step()
-    double(1)
 
     tg_own = (reach(1, 0) + reach(0, 1), reach(2, 0) + reach(1, 1))
     edge_in.wait_recv()
@@ -604,39 +631,25 @@
     for here in range(2):
         tg_out[0, here] = (tg_own[here] + edge_r[here]).astype(BF16)
 
+    pl.semaphore_wait(across_a, 2)
     pl.semaphore_wait(across_b, 2)
     step()
-    double(2)
-    step()
-    double(3)
-    step()
-    double(4)
-    step()
-    doubling[4].wait_recv()
-    sz[z] = small[4, 0] + small[4, 1]
-    turn, small_arrived = links.group(sz.at[pl.ds(0, nz - 1)], beside_z[0])
-    for k in far_first:
-        turn(sz.at[z], sz.at[z], at(x, y, (z + k) % nz, c))
     step()
     step()
-    for _ in range(2 * RING + 1):
+    added = add_up(0)
+    step()
+    added = add_up(1)
+    step()
+    added = add_up(2)
+    step()
+    step()
+    added = add_up(3)
+    for _ in range(2 * RING):
         step()
-
-    small_arrived()
-    whole = sz[0]
-    for k in range(1, nz):
-        whole = whole + sz[k]
-    s_out[...] = whole
-
+    s_out[...] = added()
     for all_across in shared:
         all_across()
 
-    def other(i, carry):
-        for k in range(len(STREAMS)):
-            square(k, 1 - c, i // RING, i % RING)
-        return carry
-
-    lax.fori_loop(0, RING * RING, other, 0)
     links.drain()
 
     @pl.when(has_outer)
@@ -645,55 +658,56 @@
         edge_out.wait_send()
 
 
-def scale_kernel(r0, r1, q, s, tg, cls_out, box_out, loss_out, cls_bias_out, box_bias_out, tg_out, stage, sem):
-    slots = stage.shape[0]
-    tower_copy = pltpu.make_async_copy(tg, tg_out, sem.at[slots])
-    tower_copy.start()
+def scale_kernel(*refs):
+    rs, refs = refs[: len(STREAMS)], refs[len(STREAMS) :]
+    s, tg, cls_out, box_out, loss_out, cls_bias_out, box_bias_out, tg_out, *refs = refs
+    stage, box_stage, loss, cls_bias, box_bias, sem, rest = refs
+    others = [
+        pltpu.make_async_copy(src, dst, rest.at[k])
+        for k, (src, dst) in enumerate((
+            (tg, tg_out), (box_stage, box_out), (loss, loss_out),
+            (cls_bias, cls_bias_out), (box_bias, box_bias_out),
+        ))
+    ]
+    others[0].start()
     rows8 = lax.broadcasted_iota(jnp.int32, (8, COLS), 0)
     bias = jnp.where(rows8 < PAD_OUTS // COLS, s[...], 0.0)
-    total = bias * bias
-    for k in range(len(STREAMS)):
-        for n in range(2 * RING * RING):
-            total = total + q[k, n // (RING * RING), n // RING % RING, n % RING]
-    total = jnp.sum(total, keepdims=True)
+    total = s[6:7, 3:4] + jnp.sum(bias * bias, keepdims=True)
     scale = lax.rsqrt(total / (OUTS * (WIDTH + 1)) + NORM_EPS)
+
+    def scaled(k, put):
+        for h in range(2):
+            for r, (start, stop) in zip(rs, STREAMS):
+                put(
+                    slice(h * HALF + start, h * HALF + stop),
+                    r[h, k // RING, k % RING].astype(F32) * scale,
+                )
+
+    def chunk(k, carry):
+        rows = pl.ds(pl.multiple_of(k * BLOCK, BLOCK), BLOCK)
+
+        def put(cols, value):
+            stage[rows, cols] = value
+
+        scaled(k, put)
+        pltpu.make_async_copy(stage.at[rows], cls_out.at[rows], sem).start()
+        return carry
+
+    def put_box(cols, value):
+        box_stage[:, cols] = value[0 : OUTS - CLS]
+
+    lax.fori_loop(0, CLS // BLOCK, chunk, 0)
+    scaled(CLS // BLOCK, put_box)
     bias = bias * scale
-    cls_bias_out[...] = bias
+    cls_bias[...] = bias
     at_row, at_lane = CLS // COLS, CLS % COLS
-    box_bias_out[...] = pltpu.roll(bias, COLS - at_lane, 1)[at_row : at_row + 1, 0 : OUTS - CLS]
-    loss_out[...] = (s[6:7, 0:1] + s[6:7, 1:2]) / s[6:7, 2:3]
-
-    count = CLS // BLOCK
-
-    def store(k):
-        return pltpu.make_async_copy(
-            stage.at[k % slots],
-            cls_out.at[pl.ds(pl.multiple_of(k * BLOCK, BLOCK), BLOCK)],
-            sem.at[k % slots],
-        )
-
-    def chunk(k, carry):
-        @pl.when(k >= slots)
-        def _():
-            store(k - slots).wait()
-
-        for h in range(2):
-            for r, (start, stop) in zip((r0, r1), STREAMS):
-                stage[k % slots, :, h * HALF + start : h * HALF + stop] = (
-                    r[h, k // RING, k % RING].astype(F32) * scale
-                )
-        store(k).start()
-        return carry
-
-    lax.fori_loop(0, count, chunk, 0)
-    for h in range(2):
-        for r, (start, stop) in zip((r0, r1), STREAMS):
-            box_out[:, h * HALF + start : h * HALF + stop] = (
-                r[h, RING - 1, RING - 1].astype(F32) * scale
-            )[0 : 4 * ANCHORS]
-    for k in range(count - slots, count):
-        store(k).wait()
-    tower_copy.wait()
+    box_bias[...] = pltpu.roll(bias, COLS - at_lane, 1)[at_row : at_row + 1, 0 : OUTS - CLS]
+    loss[...] = (s[6:7, 0:1] + s[6:7, 1:2]) / s[6:7, 2:3]
+    for copy in others[1:]:
+        copy.start()
+    pltpu.make_async_copy(stage, cls_out, sem).wait()
+    for copy in others:
+        copy.wait()
 
 
 def per_device(
@@ -721,17 +735,15 @@
         per_stream += [buf(RING - 1, BLOCK, width)] * 2
         per_stream += [buf(nz, per, COLS, dtype=F32)] + [buf(nz, per, COLS)] * 3
 
-    r0, r1, q, s, tower_grad = pl.pallas_call(
+    *rs, s, tower_grad = pl.pallas_call(
         functools.partial(step_kernel, zl_count, zh_count),
         out_shape=(
-            buf(2, RING, RING, BLOCK, STREAMS[0][1] - STREAMS[0][0]),
-            buf(2, RING, RING, BLOCK, STREAMS[1][1] - STREAMS[1][0]),
-            buf(len(STREAMS), 2, RING, RING, 8, COLS, dtype=F32),
+            *(buf(2, RING, RING, BLOCK, stop - start) for start, stop in STREAMS),
             buf(8, COLS, dtype=F32),
             buf(*tower.shape),
         ),
         in_specs=[hbm] * 8,
-        out_specs=(vmem, vmem, vmem, vmem, vmem),
+        out_specs=(vmem,) * (len(STREAMS) + 2),
         scratch_shapes=[
             buf(*tower.shape),
             buf(CLS, WIDTH),
@@ -751,13 +763,16 @@
             buf(PAD_OUTS, 2 * COLS),
             buf(PAD_OUTS, 2 * COLS),
             buf(2, PAD_OUTS - CLS, COLS, dtype=F32),
-            buf(5, 2, 8, COLS, dtype=F32),
+            buf(2, 8, COLS, dtype=F32),
+            buf(RING, 8, COLS, dtype=F32),
+            buf(RING, 8, COLS, dtype=F32),
             buf(nz, 8, COLS, dtype=F32),
             buf(2 * COLS, WIDTH, dtype=F32),
             buf(2, COLS, DEPTH, dtype=F32),
             buf(2, COLS, DEPTH, dtype=F32),
             pltpu.SemaphoreType.DMA((8,)),
             pltpu.SemaphoreType.REGULAR((max(nz // 2 - 1, 1),)),
+            pltpu.SemaphoreType.REGULAR,
             pltpu.SemaphoreType.REGULAR,
             pltpu.SemaphoreType.DMA((IN_FLIGHT + GROUPS,)),
             pltpu.SemaphoreType.DMA((RECEIVES,)),
@@ -779,15 +794,20 @@
             jax.ShapeDtypeStruct((1, OUTS - CLS), F32),
             jax.ShapeDtypeStruct(tower.shape, BF16),
         ),
-        in_specs=[vmem, vmem, vmem, vmem, vmem],
-        out_specs=(hbm, vmem, vmem, vmem, vmem, hbm),
+        in_specs=[vmem] * (len(STREAMS) + 2),
+        out_specs=(hbm,) * 6,
         scratch_shapes=[
-            buf(4, BLOCK, WIDTH, dtype=F32),
+            buf(CLS, WIDTH, dtype=F32),
+            buf(OUTS - CLS, WIDTH, dtype=F32),
+            buf(1, 1, dtype=F32),
+            buf(8, COLS, dtype=F32),
+            buf(1, OUTS - CLS, dtype=F32),
+            pltpu.SemaphoreType.DMA,
             pltpu.SemaphoreType.DMA((5,)),
         ],
         compiler_params=pltpu.CompilerParams(vmem_limit_bytes=40 * 2**20),
         name="scale",
-    )(r0, r1, q, s, tower_grad)
+    )(*rs, s, tower_grad)
     return (
         loss.reshape(()),
         cls_grad,

time: 62.9 us -> 59.4 us (0.944)
  Pallas kernels: 62.1 us -> 58.7 us
    pallas_call x1, Pallas kernels: 57.6 us -> 55.5 us  [per_device(): pl.pallas_call(functools.partial(step_kernel, zl_count, zh_count), out_sh...]
    pallas_call x1, Pallas kernels: 4.51 us -> 3.18 us  [per_device(): pl.pallas_call(scale_kernel, out_shape=(jax.ShapeDtypeStruct((CLS, WIDTH)...]
where the time goes in v5:
time: 59.4 us; the launch traced here: 59.3 us
  Pallas kernels  58.7 us (99%)
  between operations  0.64 us (1%)
    pallas_call x1, Pallas kernels, per_device(): pl.pallas_call(functools.partial(step_kernel, zl_count, zh_count), out_sh...  55.5 us
    pallas_call x1, Pallas kernels, per_device(): pl.pallas_call(scale_kernel, out_shape=(jax.ShapeDtypeStruct((CLS, WIDTH)...  3.18 us

profile of v5, /device:TPU:1, one launch (start us, length us, event | category | flops | bytes accessed | tf_op | source)
XLA Modules:
  0.0 59.3 jit_solution(8891976202503676159)
XLA Ops:
  0.6 55.5 %step.1 = (bf16[2,4,4,48,384]{4,3,2,1,0:T(8,128)(2,1)S(1)}, bf16[2,4,4,48,384]{4,3,2,1,0:T(8,128)(2,1)S(1)}, bf16[2,4,4,48,384]{4,3,2,1,0:T(8,128)(2,1)S(1)}, f3...) custom-call(bf16[1,2,128,256]{3,2,1,0:T(8,128)(2,1)} %tower_in.1, bf16[720,2304]{1,0:T(8,128)(2,1)} %wc_in.1, ...), custom_call_target="tpu_custom_call" | custom-call | tf_op jit(solution)/shard_map/step/pallas_call | solution.py:738
  56.1 3.2 %scale.1 = (f32[720,2304]{1,0:T(8,128)}, f32[36,2304]{1,0:T(8,128)}, f32[1,1]{1,0:T(1,128)}, f32[8,128]{1,0:T(8,128)}, f32[1,36]{1,0:T(1,128)}, /*index=5*/bf16[1,2,128,256]{3,2,1,0:T(8,128)(2,1)}) custom-call(bf16[2,4,4,48,384]{4,3,2,1,0:T(8,128)(2,1)S(1)} %get-tuple-element.17.refs_0_, bf16[2,4,4,48,384]{4,3,2,1,0:T(8,128)(2,1)S(1)} %get-tuple-element.18.refs_1_, ...), custom_call_target="tpu_custom_call" | custom-call | tf_op jit(solution)/shard_map/scale/pallas_call | solution.py:787

commit v6 on v5

--- a/solution.py
+++ b/solution.py
@@ -15,9 +15,9 @@
 NORM_EPS = 1e-06
 
 RING = 4
-IN_FLIGHT = 32
-RECEIVES = 85
-GROUPS = 18
+IN_FLIGHT = 16
+RECEIVES = 55
+APART = 5
 CLS = ANCHORS * CLASSES
 OUTS = CLS + 4 * ANCHORS
 PAD_OUTS = 768
@@ -40,11 +40,11 @@
 class Links:
     def __init__(self, send, recv):
         self.send, self.recv = send, recv
-        self.sends = self.recvs = 0
-        self.sent, self.groups = [], []
+        self.apart = self.recvs = 0
+        self.ring, self.kept = [], []
 
     def make(self, src, dst, device, pair=None):
-        send_id, recv_id = self.pair() if pair is None else pair
+        send_id, recv_id = self.pair(True) if pair is None else pair
         return pltpu.make_async_remote_copy(
             src_ref=src,
             dst_ref=dst,
@@ -54,25 +54,25 @@
             device_id_type=MESH,
         )
 
-    def pair(self):
-        self.sends += 1
+    def pair(self, apart):
         self.recvs += 1
-        return IN_FLIGHT + self.sends - 1, self.recvs - 1
+        if apart:
+            self.apart += 1
+            return IN_FLIGHT + self.apart - 1, self.recvs - 1
+        if len(self.ring) >= IN_FLIGHT:
+            self.ring[-IN_FLIGHT].wait_send()
+        return len(self.ring) % IN_FLIGHT, self.recvs - 1
 
     def push(self, src, dst, device):
-        slot = len(self.sent) % IN_FLIGHT
-        if len(self.sent) >= IN_FLIGHT:
-            self.sent[-IN_FLIGHT].wait_send()
-        self.recvs += 1
-        copy = self.make(src, dst, device, (slot, self.recvs - 1))
+        copy = self.make(src, dst, device, self.pair(False))
         copy.start()
-        self.sent.append(copy)
+        self.ring.append(copy)
         return copy
 
-    def group(self, whole, device):
-        pair = self.pair()
+    def group(self, whole, device, apart=False):
+        pair = self.pair(apart)
         both = self.make(whole, whole, device, pair)
-        self.groups.append(both)
+        (self.kept if apart else self.ring).append(both)
 
         def start(src, dst, to):
             self.make(src, dst, to, pair).start()
@@ -80,9 +80,7 @@
         return start, both.wait_recv
 
     def drain(self):
-        for copy in self.sent[-IN_FLIGHT:]:
-            copy.wait_send()
-        for both in self.groups:
+        for both in self.ring[-IN_FLIGHT:] + self.kept:
             both.wait_send()
 
 
@@ -208,26 +206,12 @@
     loads = [
         pltpu.make_async_copy(src, dst, load_sem.at[k])
         for k, (src, dst) in enumerate((
-            (tindex_in, tindex), (boxes_in, boxes), (tower_in, tower), (wb_in, wb),
+            (tower_in, tower), (tindex_in, tindex), (boxes_in, boxes), (wb_in, wb),
             (wc_in, w), (cls_bias_in, cls_bias), (box_bias_in, box_bias), (labels_in, labels),
         ))
     ]
     for load in loads:
         load.start()
-    for load in loads[:4]:
-        load.wait()
-
-    wanted = jnp.concatenate([tindex[0, :, 0, :], tindex[0, :, 1, :]], axis=1)
-
-    def pick(n, found):
-        hit = wanted == n
-        return tuple(jnp.where(hit, boxes[0, j, n], found[j]) for j in range(4))
-
-    zero = jnp.zeros(wanted.shape, F32)
-    corners = lax.fori_loop(0, boxes.shape[2], pick, (zero, zero, zero, zero))
-    wbs[...] = jnp.zeros(wbs.shape, BF16)
-    wbs[0 : 4 * ANCHORS, :] = wb[...]
-
     def fill(row, place, halves, put):
         value = row.astype(F32)
         for col_tap in range(3):
@@ -251,10 +235,8 @@
     def put_beside(half, rows, cols, value):
         beside[rows, cols] = value
 
-    for here in range(2):
-        ext[1 + 2 * c + here] = tower[0, here]
-        fill(tower[0, here], 1 + here, (0, 1), put_own)
-
+    wbs[...] = jnp.zeros(wbs.shape, BF16)
+    loads[0].wait()
     pl.semaphore_wait(barrier, 1 + 4 + 2 + has_outer.astype(jnp.int32))
 
     rounds = nz // 2 - 1
@@ -285,6 +267,23 @@
         pl.semaphore_signal(across_a, inc=1, device_id=ring(near, b), device_id_type=MESH)
     for near in (flip(b), 3 - b):
         pl.semaphore_signal(across_b, inc=1, device_id=ring(a, near), device_id_type=MESH)
+
+    for here in range(2):
+        ext[1 + 2 * c + here] = tower[0, here]
+        fill(tower[0, here], 1 + here, (0, 1), put_own)
+
+    for load in loads[1:4]:
+        load.wait()
+
+    wanted = jnp.concatenate([tindex[0, :, 0, :], tindex[0, :, 1, :]], axis=1)
+
+    def pick(n, found):
+        hit = wanted == n
+        return tuple(jnp.where(hit, boxes[0, j, n], found[j]) for j in range(4))
+
+    zero = jnp.zeros(wanted.shape, F32)
+    corners = lax.fori_loop(0, boxes.shape[2], pick, (zero, zero, zero, zero), unroll=5)
+    wbs[0 : 4 * ANCHORS, :] = wb[...]
 
     nt = (((1,), (1,)), ((), ()))
 
@@ -365,7 +364,15 @@
             total = total + jnp.sum(value.reshape(CLASSES // 8, 8, COLS), axis=0)
         return total
 
-    focal_sum = lax.fori_loop(0, ANCHORS, focal, jnp.zeros((8, COLS), F32))
+    glow_across, glow_arrived = links.group(theirs, sibling)
+
+    def send_grads(start, stop):
+        glow_across(glow.at[pl.ds(start, stop - start)], theirs.at[pl.ds(start, stop - start)], sibling)
+
+    focal_sum = jnp.zeros((8, COLS), F32)
+    for k in range(3):
+        focal_sum = lax.fori_loop(3 * k, 3 * k + 3, focal, focal_sum)
+        send_grads(3 * k * CLASSES, 3 * (k + 1) * CLASSES)
 
     assigned = jnp.concatenate([labels[0, :, 0, :], labels[0, :, 1, :]], axis=1)
     for here in range(2):
@@ -382,7 +389,7 @@
             boxy[here, pl.ds(j, ANCHORS, stride=4), :] = offset_grads[j][:, lanes]
         gf[CLS:PAD_OUTS, lanes] = boxy[here]
     glow[CLS:PAD_OUTS, :] = gf[CLS:PAD_OUTS, :].astype(BF16)
-    glow_across = links.push(glow, theirs, sibling)
+    send_grads(CLS, PAD_OUTS)
 
     streams = []
     each = len(per_stream) // len(STREAMS)
@@ -404,7 +411,7 @@
             for place in range(4):
                 fill(ext[2 * (1 - half) + place], place, (half,), put_beside)
 
-    glow_across.wait_recv()
+    glow_arrived()
 
     def wrap(i):
         return (i + RING) % RING
@@ -417,7 +424,7 @@
 
     def stream(
         number, r, start, stop,
-        acc, a1s, a1r, a2s, a2r, accb, b_s, b_r, zf, zs, zr, zg,
+        acc, far_s, far_r, own_s, own_r, accb, b_s, b_r, zf, zs, zr, zg,
     ):
         width = stop - start
         if number:
@@ -426,32 +433,33 @@
         acc[...] += part.reshape(acc.shape)
 
         steps = ((flip(a), 3 - a), (3 - a, flip(a)))
-        first = {}
-        for which in (1, 0):
-            for s in range(2):
-                near, far = steps[s]
-                back = (3 - near, flip(near))[s]
-                quarter = back if which else near
-                for j in range(2):
-                    a1s[s, which, j] = acc[quarter, 2 * s + j].astype(BF16)
-                first[s, which] = links.push(a1s.at[s, which], a1r.at[s, which], ring(near, b))
-        yield
-
-        second = []
+        first = []
         for s in range(2):
             near, far = steps[s]
-            first[s, 1].wait_recv()
             for j in range(2):
-                a2s[s, j] = (acc[far, 2 * s + j] + a1r[s, 1, j].astype(F32)).astype(BF16)
-            second.append(links.push(a2s.at[s], a2r.at[s], ring(far, b)))
+                far_s[s, j] = acc[(3 - near, flip(near))[s], 2 * s + j].astype(BF16)
+            first.append(links.push(far_s.at[s], far_r.at[s], ring(near, b)))
+        turn, arrived = links.group(own_r, ring(flip(a), b))
+        for s in range(2):
+            near, far = steps[s]
+            for j in range(2):
+                own_s[s, j] = acc[near, 2 * s + j].astype(BF16)
+            turn(own_s.at[s], own_r.at[s], ring(near, b))
         yield
 
         for s in range(2):
-            first[s, 0].wait_recv()
-            second[s].wait_recv()
+            near, far = steps[s]
+            first[s].wait_recv()
+            for j in range(2):
+                own_s[2 + s, j] = (acc[far, 2 * s + j] + far_r[s, j].astype(F32)).astype(BF16)
+            turn(own_s.at[2 + s], own_r.at[2 + s], ring(far, b))
+        yield
+
+        arrived()
+        for s in range(2):
             for j in range(2):
                 accb[2 * s + j] = (
-                    acc[a, 2 * s + j] + a1r[s, 0, j].astype(F32) + a2r[s, j].astype(F32)
+                    acc[a, 2 * s + j] + own_r[s, j].astype(F32) + own_r[2 + s, j].astype(F32)
                 )
 
         turn, arrived = links.group(b_r, ring(a, wrap(b + 1)))
@@ -497,7 +505,7 @@
                 pieces.append(zf[n // per, (n % per) * 8 : (n % per) * 8 + 8, :])
             r[c, a, b, :, k * COLS : (k + 1) * COLS] = jnp.concatenate(pieces, axis=0).astype(BF16)
 
-        across, all_across = links.group(r.at[1 - c], sibling)
+        across, all_across = links.group(r.at[1 - c], sibling, apart=True)
         shared.append(all_across)
 
         def share(a_, b_):
@@ -505,24 +513,30 @@
 
         def along_a(b_):
             block = r.at[c, a, b_]
-            return (
-                links.push(block, block, ring(wrap(a + 1), b)),
-                links.push(block, block, ring(wrap(a - 1), b)),
-            )
+            turn, arrived = links.group(r.at[c, a, pl.ds(0, 2)], ring(wrap(a + 1), b))
+            turn(block, block, ring(wrap(a + 1), b))
+            turn(block, block, ring(wrap(a - 1), b))
+            return arrived
 
         block = r.at[c, a, b]
         wide = [along_a(b)]
-        to = {k: links.push(block, block, ring(a, wrap(b + k))) for k in (1, 3, 2)}
+        turn, arrived = links.group(r.at[c, a, pl.ds(0, 2)], ring(a, wrap(b + 1)))
+        for k in (1, 3):
+            turn(block, block, ring(a, wrap(b + k)))
         share(a, b)
         yield
 
+        arrived()
+        turn, arrived = links.group(r.at[c, a, b], ring(a, wrap(b + 1)))
+        for k, rows in ((1, slice(0, 32)), (3, slice(32, BLOCK))):
+            block = r.at[c, a, wrap(b - k), rows]
+            turn(block, block, ring(a, wrap(b + k)))
         for k in (1, 3):
-            to[k].wait_recv()
             wide.append(along_a(wrap(b - k)))
             share(a, wrap(b - k))
         yield
 
-        to[2].wait_recv()
+        arrived()
         wide.append(along_a(wrap(b + 2)))
         share(a, wrap(b + 2))
         yield
@@ -530,27 +544,27 @@
         order = (b, wrap(b - 1), wrap(b + 1), wrap(b + 2))
         rest = []
         for k, b_ in enumerate(order):
-            wide[k][0].wait_recv()
-            if k < 2:
-                block = r.at[c, wrap(a - 1), b_]
-                rest.append(links.push(block, block, ring(wrap(a + 1), b)))
+            wide[k]()
+            step = -1 if k < 2 else 1
+            if k % 2 == 0:
+                turn, arrived = links.group(r.at[c, a, pl.ds(0, 2)], ring(wrap(a - step), b))
+                rest.append(arrived)
+            block = r.at[c, wrap(a + step), b_]
+            turn(block, block, ring(wrap(a - step), b))
             share(wrap(a - 1), b_)
-            wide[k][1].wait_recv()
-            if k >= 2:
-                block = r.at[c, wrap(a + 1), b_]
-                rest.append(links.push(block, block, ring(wrap(a - 1), b)))
             share(wrap(a + 1), b_)
             yield
-        for k, b_ in enumerate(order):
-            rest[k].wait_recv()
-            share(wrap(a + 2), b_)
+        for k in range(2):
+            rest[k]()
+            for b_ in order[2 * k : 2 * k + 2]:
+                share(wrap(a + 2), b_)
             yield
 
     going = [stream(k, *refs) for k, refs in enumerate(streams)]
 
-    def step():
-        for one in going:
-            next(one, None)
+    def step(*numbers):
+        for k in numbers or range(len(going)):
+            next(going[k], None)
 
     step()
     hear(2)
@@ -644,7 +658,7 @@
     step()
     step()
     added = add_up(3)
-    for _ in range(2 * RING):
+    for _ in range(RING + 2):
         step()
     s_out[...] = added()
     for all_across in shared:
@@ -726,10 +740,10 @@
         per = -(-(BLOCK // 8 * (width // COLS)) // nz) * 8
         per_stream += [
             buf(RING, RING, BLOCK, width, dtype=F32),
-            buf(2, 2, 2, BLOCK, width),
-            buf(2, 2, 2, BLOCK, width),
             buf(2, 2, BLOCK, width),
             buf(2, 2, BLOCK, width),
+            buf(4, 2, BLOCK, width),
+            buf(4, 2, BLOCK, width),
             buf(RING, BLOCK, width, dtype=F32),
         ]
         per_stream += [buf(RING - 1, BLOCK, width)] * 2
@@ -774,7 +788,7 @@
             pltpu.SemaphoreType.REGULAR((max(nz // 2 - 1, 1),)),
             pltpu.SemaphoreType.REGULAR,
             pltpu.SemaphoreType.REGULAR,
-            pltpu.SemaphoreType.DMA((IN_FLIGHT + GROUPS,)),
+            pltpu.SemaphoreType.DMA((IN_FLIGHT + APART,)),
             pltpu.SemaphoreType.DMA((RECEIVES,)),
             *per_stream,
         ],

time: 59.4 us -> 58.7 us (0.988)
  Pallas kernels: 58.7 us -> 58 us
    pallas_call x1, Pallas kernels: 55.5 us -> 54.8 us  [per_device(): pl.pallas_call(functools.partial(step_kernel, zl_count, zh_count), out_sh...]
where the time goes in v6:
time: 58.7 us; the launch traced here: 58.6 us
  Pallas kernels  58 us (99%)
  between operations  0.64 us (1%)
    pallas_call x1, Pallas kernels, per_device(): pl.pallas_call(functools.partial(step_kernel, zl_count, zh_count), out_sh...  54.8 us
    pallas_call x1, Pallas kernels, per_device(): pl.pallas_call(scale_kernel, out_shape=(jax.ShapeDtypeStruct((CLS, WIDTH)...  3.18 us

profile of v6, /device:TPU:1, one launch (start us, length us, event | category | flops | bytes accessed | tf_op | source)
XLA Modules:
  0.0 58.6 jit_solution(2090111147913265401)
XLA Ops:
  0.6 54.8 %step.1 = (bf16[2,4,4,48,384]{4,3,2,1,0:T(8,128)(2,1)S(1)}, bf16[2,4,4,48,384]{4,3,2,1,0:T(8,128)(2,1)S(1)}, bf16[2,4,4,48,384]{4,3,2,1,0:T(8,128)(2,1)S(1)}, f3...) custom-call(bf16[1,2,128,256]{3,2,1,0:T(8,128)(2,1)} %tower_in.1, bf16[720,2304]{1,0:T(8,128)(2,1)} %wc_in.1, ...), custom_call_target="tpu_custom_call" | custom-call | tf_op jit(solution)/shard_map/step/pallas_call | solution.py:752
  55.5 3.2 %scale.1 = (f32[720,2304]{1,0:T(8,128)}, f32[36,2304]{1,0:T(8,128)}, f32[1,1]{1,0:T(1,128)}, f32[8,128]{1,0:T(8,128)}, f32[1,36]{1,0:T(1,128)}, /*index=5*/bf16[1,2,128,256]{3,2,1,0:T(8,128)(2,1)}) custom-call(bf16[2,4,4,48,384]{4,3,2,1,0:T(8,128)(2,1)S(1)} %get-tuple-element.17.refs_0_, bf16[2,4,4,48,384]{4,3,2,1,0:T(8,128)(2,1)S(1)} %get-tuple-element.18.refs_1_, ...), custom_call_target="tpu_custom_call" | custom-call | tf_op jit(solution)/shard_map/scale/pallas_call | solution.py:801

commit v7 on v6

--- a/solution.py
+++ b/solution.py
@@ -16,7 +16,7 @@
 
 RING = 4
 IN_FLIGHT = 16
-RECEIVES = 55
+RECEIVES = 61
 APART = 5
 CLS = ANCHORS * CLASSES
 OUTS = CLS + 4 * ANCHORS
@@ -429,16 +429,19 @@
         width = stop - start
         if number:
             own_part(number)
-        part = jnp.dot(theirs[...], beside[:, start:stop], preferred_element_type=F32)
-        acc[...] += part.reshape(acc.shape)
 
         steps = ((flip(a), 3 - a), (3 - a, flip(a)))
         first = []
         for s in range(2):
             near, far = steps[s]
+            back = (3 - near, flip(near))[s]
+            rows = pl.ds(pl.multiple_of((back * RING + 2 * s) * BLOCK, 2 * BLOCK), 2 * BLOCK)
+            part = jnp.dot(theirs[rows, :], beside[:, start:stop], preferred_element_type=F32)
             for j in range(2):
-                far_s[s, j] = acc[(3 - near, flip(near))[s], 2 * s + j].astype(BF16)
+                far_s[s, j] = (acc[back, 2 * s + j] + part[j * BLOCK : (j + 1) * BLOCK]).astype(BF16)
             first.append(links.push(far_s.at[s], far_r.at[s], ring(near, b)))
+        part = jnp.dot(theirs[...], beside[:, start:stop], preferred_element_type=F32)
+        acc[...] += part.reshape(acc.shape)
         turn, arrived = links.group(own_r, ring(flip(a), b))
         for s in range(2):
             near, far = steps[s]
@@ -546,18 +549,14 @@
         for k, b_ in enumerate(order):
             wide[k]()
             step = -1 if k < 2 else 1
-            if k % 2 == 0:
-                turn, arrived = links.group(r.at[c, a, pl.ds(0, 2)], ring(wrap(a - step), b))
-                rest.append(arrived)
             block = r.at[c, wrap(a + step), b_]
-            turn(block, block, ring(wrap(a - step), b))
+            rest.append(links.push(block, block, ring(wrap(a - step), b)))
             share(wrap(a - 1), b_)
             share(wrap(a + 1), b_)
             yield
-        for k in range(2):
-            rest[k]()
-            for b_ in order[2 * k : 2 * k + 2]:
-                share(wrap(a + 2), b_)
+        for copy, b_ in zip(rest, order):
+            copy.wait_recv()
+            share(wrap(a + 2), b_)
             yield
 
     going = [stream(k, *refs) for k, refs in enumerate(streams)]
@@ -658,7 +657,7 @@
     step()
     step()
     added = add_up(3)
-    for _ in range(RING + 2):
+    for _ in range(2 * RING):
         step()
     s_out[...] = added()
     for all_across in shared:

time: 58.7 us -> 58.9 us (level)
  no operation moved by 1% of the time
where the time goes in v7:
time: 58.9 us; the launch traced here: 58.8 us
  Pallas kernels  58.1 us (99%)
  between operations  0.64 us (1%)
    pallas_call x1, Pallas kernels, per_device(): pl.pallas_call(functools.partial(step_kernel, zl_count, zh_count), out_sh...  55 us
    pallas_call x1, Pallas kernels, per_device(): pl.pallas_call(scale_kernel, out_shape=(jax.ShapeDtypeStruct((CLS, WIDTH)...  3.18 us

profile of v7, /device:TPU:1, one launch (start us, length us, event | category | flops | bytes accessed | tf_op | source)
XLA Modules:
  0.0 58.8 jit_solution(10962656999066997045)
XLA Ops:
  0.6 55.0 %step.1 = (bf16[2,4,4,48,384]{4,3,2,1,0:T(8,128)(2,1)S(1)}, bf16[2,4,4,48,384]{4,3,2,1,0:T(8,128)(2,1)S(1)}, bf16[2,4,4,48,384]{4,3,2,1,0:T(8,128)(2,1)S(1)}, f3...) custom-call(bf16[1,2,128,256]{3,2,1,0:T(8,128)(2,1)} %tower_in.1, bf16[720,2304]{1,0:T(8,128)(2,1)} %wc_in.1, ...), custom_call_target="tpu_custom_call" | custom-call | tf_op jit(solution)/shard_map/step/pallas_call | solution.py:751
  55.6 3.2 %scale.1 = (f32[720,2304]{1,0:T(8,128)}, f32[36,2304]{1,0:T(8,128)}, f32[1,1]{1,0:T(1,128)}, f32[8,128]{1,0:T(8,128)}, f32[1,36]{1,0:T(1,128)}, /*index=5*/bf16[1,2,128,256]{3,2,1,0:T(8,128)(2,1)}) custom-call(bf16[2,4,4,48,384]{4,3,2,1,0:T(8,128)(2,1)S(1)} %get-tuple-element.17.refs_0_, bf16[2,4,4,48,384]{4,3,2,1,0:T(8,128)(2,1)S(1)} %get-tuple-element.18.refs_1_, ...), custom_call_target="tpu_custom_call" | custom-call | tf_op jit(solution)/shard_map/scale/pallas_call | solution.py:800
